TPU v7x, 32 devices: a whole 2x2x4 slice. The times are simulated.
32 devices in a mesh: layer: 8 (over z, x), split: 4 (over y, core).
Axes of the slice: x: 2, y: 2, z: 4, core: 2. Of those that a mesh axis runs over, the one named last changes fastest.
Arguments:
- right_side: float32 [32, 512, 128], P('layer', 'split'), may hold values from -6 to 6
- diagonal: float32 [32, 512, 128], P('layer', 'split'), may hold values from 0.1 to 1
- inverses: float32 [32, 512, 512], P('layer', None, 'split'), may hold values from -1 to 1, as said below
Outputs:
- solution_field: float32 [32, 512, 128], P('layer', 'split')
- residual: float32 [32, 512, 128], P('layer', 'split')
Inputs may be any that keep to these rules, and one draw needn't show every extreme that they name: `inverses`: each plane's inverse is a diagonal matrix with entries between 0.5 and 1 plus a dense coupling with zero diagonal and spectral norm below 0.2.
All inputs are finite; a program needn't handle non-finite values.
Results may differ from a plain program's by a relative error of at most 0.0003.
Values sent between devices are 32-bit elements; how exact they have to be, the bound alone decides.
A program may use at most 64 MiB of HBM per device.

v0:
```python
import jax
import jax.numpy as jnp
from jax import lax
from jax.sharding import PartitionSpec as P


def with_halo(x, sides, width):
    for axis, dim in sides:
        size, length = (lax.axis_size(axis), x.shape[dim])
        up = [(i, (i + 1) % size) for i in range(size - 1)]
        down = [(j, i) for i, j in up]
        last = lax.slice_in_dim(x, length - width, length, axis=dim)
        first = lax.slice_in_dim(x, 0, width, axis=dim)
        before = lax.ppermute(last, axis, up)
        after = lax.ppermute(first, axis, down)
        x = jnp.concatenate([before, x, after], axis=dim)
    return x


def from_behind(block, axis, distance):
    devices = range(lax.axis_size(axis))
    route = [(i - distance, i) for i in devices if i - distance in devices]
    return lax.ppermute(block, axis, route)


def stencil(values, diagonal):
    padded = with_halo(values, (("layer", 0), ("split", 1)), 1)
    beside = padded[2:, 1:-1, :] + padded[:-2, 1:-1, :]
    beside = beside + padded[1:-1, 2:, :] + padded[1:-1, :-2, :]
    centre_part = padded[1:-1, 1:-1, :]
    y_upper = jnp.pad(centre_part[:, :, 1:], ((0, 0), (0, 0), (0, 1)))
    y_lower = jnp.pad(centre_part[:, :, :-1], ((0, 0), (0, 0), (1, 0)))
    return (6.0 + diagonal) * values - beside - y_upper - y_lower


def down_local(matrices, portion, carried):

    def down_advance(state, inputs):
        matrix, source = inputs
        state = jnp.dot(matrix, source + state, precision=lax.Precision.HIGHEST)
        return (state, state)

    return lax.scan(down_advance, carried, (matrices, portion))


def up_local(matrices, portion, carried):

    def up_advance(state, inputs):
        matrix, below = inputs
        state = below + jnp.dot(matrix, state, precision=lax.Precision.HIGHEST)
        return (state, state)

    return lax.scan(up_advance, carried, (matrices, portion), reverse=True)


def chain_sweep(sweep_fn, matrices, source, sender, anchor, nblocks):
    depth_count = lax.axis_size("layer")
    block_width = source.shape[2] // nblocks
    plane_shape = (source.shape[1], block_width)
    result = jnp.zeros_like(source)
    incoming = jnp.zeros(plane_shape, jnp.float32)

    def chain_advance(turn, state):
        result, incoming = state
        block_raw = turn - anchor
        active = jnp.logical_and(block_raw >= 0, block_raw < nblocks)

        def working(unused):
            return sweep_fn(matrices, source, incoming)

        def resting(unused):
            return (jnp.zeros(plane_shape, jnp.float32), jnp.zeros_like(source))

        outgoing, stacked = lax.cond(active, working, resting, None)
        previous = result
        result = jnp.where(active, stacked, previous)
        return (result, sender(outgoing))

    result, incoming = lax.fori_loop(
        0, depth_count + nblocks - 1, chain_advance, (result, incoming)
    )
    return result


def per_device(right_side, diagonal, inverses):
    matrices = lax.all_gather(inverses, "split", axis=2, tiled=True)
    columns = lax.all_to_all(right_side, "split", split_axis=2, concat_axis=1, tiled=True)
    nblocks = 1
    own_index = lax.axis_index("layer")
    depth_count = lax.axis_size("layer")
    applied_rhs = stencil(right_side, diagonal)

    def send_down(values):
        return from_behind(values, "layer", 1)

    def send_up(values):
        return from_behind(values, "layer", -1)

    lower_sweep = chain_sweep(down_local, matrices, columns, send_down, own_index, nblocks)
    upper_sweep = chain_sweep(
        up_local, matrices, lower_sweep, send_up, depth_count - 1 - own_index, nblocks
    )
    direction = lax.all_to_all(upper_sweep, "split", split_axis=1, concat_axis=2, tiled=True)
    image = stencil(direction, diagonal)
    applied_image = stencil(image, diagonal)
    sums_all = lax.psum(
        (
            jnp.sum(right_side * right_side),
            jnp.sum(right_side * image),
            jnp.sum(applied_rhs * right_side),
            jnp.sum(applied_rhs * image),
            jnp.sum(applied_image * right_side),
            jnp.sum(applied_image * image),
            jnp.sum(applied_rhs * applied_rhs),
            jnp.sum(applied_rhs * applied_image),
            jnp.sum(applied_image * applied_image),
        ),
        ("layer", "split"),
    )
    (
        norm_sq,
        curv_sum,
        rhs_rhs,
        rhs_image,
        image_rhs,
        image_image,
        arhs_arhs,
        arhs_aimage,
        aimage_aimage,
    ) = sums_all
    step_alpha = norm_sq / curv_sum
    middle = right_side - step_alpha * image
    tangent = applied_rhs - step_alpha * applied_image
    cross_sum = (
        rhs_rhs - step_alpha * (rhs_image + image_rhs) + step_alpha * step_alpha * image_image
    )
    self_sum = arhs_arhs - 2.0 * step_alpha * arhs_aimage + step_alpha * step_alpha * aimage_aimage
    step_omega = cross_sum / self_sum
    solution_field = step_alpha * direction + step_omega * middle
    residual = middle - step_omega * tangent
    return (solution_field, residual)


def solution(mesh):
    placed = (P("layer", "split", None), P("layer", "split", None), P("layer", None, "split"))
    return jax.shard_map(
        per_device,
        mesh=mesh,
        in_specs=placed,
        out_specs=(P("layer", "split", None), P("layer", "split", None)),
        check_vma=False,
    )
```

profile of v0, /device:TPU:0, one launch (start us, length us, event | category | flops | bytes accessed | tf_op | source)
XLA Modules:
  0.0 438.2 jit_solution(2182941142321325081)
XLA Ops:
  9.7 4.3 all-to-all-start
  16.4 4.7 %collective-permute-start.7 = (f32[1,128,128]{1,2,0:T(8,128)S(1)}, f32[1,128,128]{1,2,0:T(8,128)S(1)}, u32[]{:S(2)}, u32[]{:S(2)}) collective-permute-start(f32[1,128,128]{1,2,0:T(8,128)S(1)} %get-tuple-element.506), channel_id=1, source_target_pairs={{0,4},{4,8},{8,12},{12,16},{16,20},{20,24},{24,28},{1,5},{5,9},{9,... | collective-permute-start | bytes 196616 | tf_op jit(solution)/shard_map/ppermute | solution.py:14
  23.9 23.4 %all-gather.2.cloned.1.call-done = f32[4,512,512]{2,1,0:T(8,128)} async-done(((f32[4,512,128]{2,1,0:T(8,128)}), f32[4,512,512]{2,1,0:T(8,128)}) %all-gather.2.cloned.1.call-update) | async-done | bytes 4194320 | tf_op jit(solution)/shard_map/all_gather | solution.py:86
  47.3 102.0 %while.60 = (s32[]{:T(128)}, f32[4,512,32]{1,2,0:T(8,128)S(1)}, f32[512,32]{0,1:T(8,128)S(1)}, s32[]{:T(128)}, f32[4,512,512]{2,1,0:T(8,128)}, /*index=5*/f32[4,512,32]{1,2,0:T(8,128)S(1)}, s32[]{:T(128)}, s32[]{:T(128)}) while((s32[]{:T(128)}, f32[4,512,32]{1,2,0:T(8,128)S(1)}, f32[512,32]{0,1:T(8,128)S(1)}, s32[]{:T(128)}, ...), condition=%wide.region_7.8_spmd.clone, body=%wide.region_2.7_spmd.clone.sunk | while | flops 100810760 | bytes 2623315 | solution.py:79
  47.3 11.7 %conditional.6 = (f32[512,32]{0,1:T(8,128)S(1)}, f32[4,512,32]{1,2,0:T(8,128)}) conditional(s32[]{:T(128)} %convert_element_type.26, () %tuple.150, (f32[4,512,512]{2,1,0:T(8,128)}, f32[4,512,32]{1,2,0:T(8,128)S(1)}, f32[512,32]{0,1:T(8,128)S(1)}) %tuple.151), branch_computations={%region_3.3_spmd, %region_4.6_spmd} | conditional | flops 100679680 | bytes 1574541 | solution.py:74
  47.3 11.7 %while.58 = (s32[]{:T(128)}, f32[512,32]{0,1:T(8,128)S(1)}, f32[4,512,32]{1,2,0:T(8,128)}, f32[4,512,512]{2,1,0:T(8,128)}, f32[4,512,32]{1,2,0:T(8,128)S(1)}, /*index=5*/s32[]{:T(128)}) while((s32[]{:T(128)}, f32[512,32]{0,1:T(8,128)S(1)}, f32[4,512,32]{1,2,0:T(8,128)}, f32[4,512,512]{2,1,0:T(8,128)}, f32[4,512,32]{1,2,0:T(8,128)S(1)}, ...), condition=%wide.region_6.5_spmd, body=%wide.region_5.4_spmd.sunk | while | flops 100679680 | bytes 1443397 | solution.py:43
  63.1 15.4 %collective-permute-start.1 = (f32[512,32]{0,1:T(8,128)S(1)}, f32[512,32]{0,1:T(8,128)S(1)}, u32[]{:S(2)}, u32[]{:S(2)}) collective-permute-start(f32[512,32]{0,1:T(8,128)S(1)} %get-tuple-element.643), channel_id=1, source_target_pairs={{0,4},{4,8},{8,12},{12,16},{16,20},{20,24},{24,28},{1,5},{5,9},{9,... | collective-permute-start | bytes 196616 | tf_op jit(solution)/shard_map/while/body/eval_jaxpr/ppermute | solution.py:23
  81.1 4.3 collective-permute-start.1
  87.9 13.8 %collective-permute-start.1 = (f32[512,32]{0,1:T(8,128)S(1)}, f32[512,32]{0,1:T(8,128)S(1)}, u32[]{:S(2)}, u32[]{:S(2)}) collective-permute-start(f32[512,32]{0,1:T(8,128)S(1)} %get-tuple-element.643), channel_id=1, source_target_pairs={{0,4},{4,8},{8,12},{12,16},{16,20},{20,24},{24,28},{1,5},{5,9},{9,... | collective-permute-start | bytes 196616 | tf_op jit(solution)/shard_map/while/body/eval_jaxpr/ppermute | solution.py:23
  104.4 5.2 %collective-permute-start.1 = (f32[512,32]{0,1:T(8,128)S(1)}, f32[512,32]{0,1:T(8,128)S(1)}, u32[]{:S(2)}, u32[]{:S(2)}) collective-permute-start(f32[512,32]{0,1:T(8,128)S(1)} %get-tuple-element.643), channel_id=1, source_target_pairs={{0,4},{4,8},{8,12},{12,16},{16,20},{20,24},{24,28},{1,5},{5,9},{9,... | collective-permute-start | bytes 196616 | tf_op jit(solution)/shard_map/while/body/eval_jaxpr/ppermute | solution.py:23
  112.1 12.0 %collective-permute-start.1 = (f32[512,32]{0,1:T(8,128)S(1)}, f32[512,32]{0,1:T(8,128)S(1)}, u32[]{:S(2)}, u32[]{:S(2)}) collective-permute-start(f32[512,32]{0,1:T(8,128)S(1)} %get-tuple-element.643), channel_id=1, source_target_pairs={{0,4},{4,8},{8,12},{12,16},{16,20},{20,24},{24,28},{1,5},{5,9},{9,... | collective-permute-start | bytes 196616 | tf_op jit(solution)/shard_map/while/body/eval_jaxpr/ppermute | solution.py:23
  126.8 5.2 %collective-permute-start.1 = (f32[512,32]{0,1:T(8,128)S(1)}, f32[512,32]{0,1:T(8,128)S(1)}, u32[]{:S(2)}, u32[]{:S(2)}) collective-permute-start(f32[512,32]{0,1:T(8,128)S(1)} %get-tuple-element.643), channel_id=1, source_target_pairs={{0,4},{4,8},{8,12},{12,16},{16,20},{20,24},{24,28},{1,5},{5,9},{9,... | collective-permute-start | bytes 196616 | tf_op jit(solution)/shard_map/while/body/eval_jaxpr/ppermute | solution.py:23
  134.6 12.9 %collective-permute-start.1 = (f32[512,32]{0,1:T(8,128)S(1)}, f32[512,32]{0,1:T(8,128)S(1)}, u32[]{:S(2)}, u32[]{:S(2)}) collective-permute-start(f32[512,32]{0,1:T(8,128)S(1)} %get-tuple-element.643), channel_id=1, source_target_pairs={{0,4},{4,8},{8,12},{12,16},{16,20},{20,24},{24,28},{1,5},{5,9},{9,... | collective-permute-start | bytes 196616 | tf_op jit(solution)/shard_map/while/body/eval_jaxpr/ppermute | solution.py:23
  149.3 177.3 %while.61 = (s32[]{:T(128)}, f32[4,512,32]{1,2,0:T(8,128)S(1)}, f32[512,32]{0,1:T(8,128)S(1)}, s32[]{:T(128)}, f32[4,512,32]{1,2,0:T(8,128)S(1)}, /*index=5*/f32[4,512,512]{2,1,0:T(8,128)}, s32[]{:T(128)}, s32[]{:T(128)}) while((s32[]{:T(128)}, f32[4,512,32]{1,2,0:T(8,128)S(1)}, f32[512,32]{0,1:T(8,128)S(1)}, s32[]{:T(128)}, ...), condition=%wide.region_13.14_spmd.clone, body=%wide.region_8.13_spmd.clone.sunk | while | flops 100810760 | bytes 2884979 | solution.py:79
  151.5 6.0 %collective-permute-done = f32[512,32]{0,1:T(8,128)S(1)} collective-permute-done((f32[512,32]{0,1:T(8,128)S(1)}, f32[512,32]{0,1:T(8,128)S(1)}, u32[]{:S(2)}, u32[]{:S(2)}) %collective-permute-start) | collective-permute-done | bytes 65568 | tf_op jit(solution)/shard_map/while/body/eval_jaxpr/ppermute | solution.py:23
  159.6 13.5 %collective-permute-done = f32[512,32]{0,1:T(8,128)S(1)} collective-permute-done((f32[512,32]{0,1:T(8,128)S(1)}, f32[512,32]{0,1:T(8,128)S(1)}, u32[]{:S(2)}, u32[]{:S(2)}) %collective-permute-start) | collective-permute-done | bytes 65568 | tf_op jit(solution)/shard_map/while/body/eval_jaxpr/ppermute | solution.py:23
  175.2 5.6 %collective-permute-done = f32[512,32]{0,1:T(8,128)S(1)} collective-permute-done((f32[512,32]{0,1:T(8,128)S(1)}, f32[512,32]{0,1:T(8,128)S(1)}, u32[]{:S(2)}, u32[]{:S(2)}) %collective-permute-start) | collective-permute-done | bytes 65568 | tf_op jit(solution)/shard_map/while/body/eval_jaxpr/ppermute | solution.py:23
  183.0 14.1 %collective-permute-done = f32[512,32]{0,1:T(8,128)S(1)} collective-permute-done((f32[512,32]{0,1:T(8,128)S(1)}, f32[512,32]{0,1:T(8,128)S(1)}, u32[]{:S(2)}, u32[]{:S(2)}) %collective-permute-start) | collective-permute-done | bytes 65568 | tf_op jit(solution)/shard_map/while/body/eval_jaxpr/ppermute | solution.py:23
  199.2 5.6 %collective-permute-done = f32[512,32]{0,1:T(8,128)S(1)} collective-permute-done((f32[512,32]{0,1:T(8,128)S(1)}, f32[512,32]{0,1:T(8,128)S(1)}, u32[]{:S(2)}, u32[]{:S(2)}) %collective-permute-start) | collective-permute-done | bytes 65568 | tf_op jit(solution)/shard_map/while/body/eval_jaxpr/ppermute | solution.py:23
  207.0 12.6 %collective-permute-done = f32[512,32]{0,1:T(8,128)S(1)} collective-permute-done((f32[512,32]{0,1:T(8,128)S(1)}, f32[512,32]{0,1:T(8,128)S(1)}, u32[]{:S(2)}, u32[]{:S(2)}) %collective-permute-start) | collective-permute-done | bytes 65568 | tf_op jit(solution)/shard_map/while/body/eval_jaxpr/ppermute | solution.py:23
  221.7 86.4 %collective-permute-done = f32[512,32]{0,1:T(8,128)S(1)} collective-permute-done((f32[512,32]{0,1:T(8,128)S(1)}, f32[512,32]{0,1:T(8,128)S(1)}, u32[]{:S(2)}, u32[]{:S(2)}) %collective-permute-start) | collective-permute-done | bytes 65568 | tf_op jit(solution)/shard_map/while/body/eval_jaxpr/ppermute | solution.py:23
  308.1 12.4 %conditional.7 = (f32[512,32]{0,1:T(8,128)S(1)}, f32[4,512,32]{1,2,0:T(8,128)}) conditional(s32[]{:T(128)} %convert_element_type.27, () %tuple.153, (f32[4,512,32]{1,2,0:T(8,128)S(1)}, f32[4,512,512]{2,1,0:T(8,128)}, f32[512,32]{0,1:T(8,128)S(1)}) %tuple.154), branch_computations={%region_9.9_spmd, %region_10.12_spmd} | conditional | flops 100679680 | bytes 1836205 | solution.py:74
  308.8 11.7 %while.59 = (s32[]{:T(128)}, f32[512,32]{0,1:T(8,128)S(1)}, f32[4,512,32]{1,2,0:T(8,128)}, f32[4,512,32]{1,2,0:T(8,128)S(1)}, f32[4,512,512]{2,1,0:T(8,128)}, /*index=5*/s32[]{:T(128)}, s32[]{:T(128)}) while((s32[]{:T(128)}, f32[512,32]{0,1:T(8,128)S(1)}, f32[4,512,32]{1,2,0:T(8,128)}, f32[4,512,32]{1,2,0:T(8,128)S(1)}, ...), condition=%wide.region_12.11_spmd, body=%wide.region_11.10_spmd.sunk | while | flops 100679680 | bytes 1442905 | solution.py:53
  322.8 3.8 collective-permute-done
  328.4 3.4 all-to-all-start.1
  331.9 5.9 %all-to-all-done.1 = f32[4,1,16384]{2,1,0:T(1,128)S(1)} async-done(((f32[4,1,16384]{2,1,0:T(1,128)}), f32[4,1,16384]{2,1,0:T(1,128)S(1)}, u32[]{:S(2)}, u32[]{:S(2)}) %all-to-all-start.1) | async-done | bytes 262176 | tf_op jit(solution)/shard_map/all_to_all | solution.py:103
  341.9 4.5 %collective-permute-start.3 = (f32[1,128,128]{1,2,0:T(8,128)S(1)}, f32[1,128,128]{1,2,0:T(8,128)S(1)}, u32[]{:S(2)}, u32[]{:S(2)}) collective-permute-start(f32[1,128,128]{1,2,0:T(8,128)S(1)} %bitcast.61), channel_id=1, source_target_pairs={{0,4},{4,8},{8,12},{12,16},{16,20},{20,24},{24,28},{1,5},{5,9},{9,... | collective-permute-start | bytes 196616 | tf_op jit(solution)/shard_map/ppermute | solution.py:14
  349.9 3.1 collective-permute-start.5
  355.9 4.9 %collective-permute-start.11 = (f32[1,128,128]{1,2,0:T(8,128)S(1)}, f32[1,128,128]{1,2,0:T(8,128)S(1)}, u32[]{:S(2)}, u32[]{:S(2)}) collective-permute-start(f32[1,128,128]{1,2,0:T(8,128)S(1)} %get-tuple-element.502), channel_id=1, source_target_pairs={{0,4},{4,8},{8,12},{12,16},{16,20},{20,24},{24,28},{1,5},{5,9},{9,... | collective-permute-start | bytes 196616 | tf_op jit(solution)/shard_map/ppermute | solution.py:14
  362.2 5.7 %collective-permute-start.9 = (f32[6,1,128]{1,2,0:T(8,128)S(1)}, f32[6,1,128]{1,2,0:T(8,128)S(1)}, u32[]{:S(2)}, u32[]{:S(2)}) collective-permute-start(f32[6,1,128]{1,2,0:T(8,128)S(1)} %get-tuple-element.499), channel_id=1, source_target_pairs={{0,1},{1,2},{2,3},{4,5},{5,6},{6,7},{8,9},{9,10},{10,11},{12,13},{... | collective-permute-start | bytes 9224 | tf_op jit(solution)/shard_map/ppermute | solution.py:14
  369.5 5.3 %collective-permute-start.13 = (f32[6,1,128]{1,2,0:T(8,128)S(1)}, f32[6,1,128]{1,2,0:T(8,128)S(1)}, u32[]{:S(2)}, u32[]{:S(2)}) collective-permute-start(f32[6,1,128]{1,2,0:T(8,128)S(1)} %get-tuple-element.497), channel_id=1, source_target_pairs={{0,1},{1,2},{2,3},{4,5},{5,6},{6,7},{8,9},{9,10},{10,11},{12,13},{... | collective-permute-start | bytes 9224 | tf_op jit(solution)/shard_map/ppermute | solution.py:14
  378.5 45.9 %all-reduce.6 = (f32[]{:T(128)}, f32[]{:T(128)}, f32[]{:T(128)}, f32[]{:T(128)}, f32[]{:T(128)}, /*index=5*/f32[]{:T(128)}, f32[]{:T(128)}, f32[]{:T(128)}) all-reduce(f32[]{:T(128)} %get-tuple-element.434, f32[]{:T(128)} %multiply_reduce_fusion.8, f32[]{:T(128)} %get-tuple-element.433, ...), channel_id=1, replica_groups=mesh['layer'=8,'split'=4] {'layer','split'}, use_global_device_ids=true, to_apply=%region_17.18 | all-reduce | flops 8 | bytes 64 | tf_op jit(solution)/shard_map/psum | solution.py:106
  (152 shorter events, 100.2 us)
Async XLA Ops:
  7.2 40.1 %all-gather.2.cloned.1.call-start = ((), (), s32[]{:S(2)}) async-start(), calls=%async_computation.2 | async-start | bytes 5242880 | tf_op jit(solution)/shard_map/all_gather | solution.py:86
  9.7 14.2 %all-to-all-start = ((f32[4,128,128]{1,0,2:T(4,128)}), f32[4,128,128]{1,0,2:T(4,128)S(1)}, u32[]{:S(2)}, u32[]{:S(2)}) async-start(f32[4,128,128]{1,0,2:T(4,128)} %copy.44), calls=%async_computation | async-start | bytes 524288 | tf_op jit(solution)/shard_map/all_to_all | solution.py:87
  15.1 331.4 %collective-permute-start.6 = (f32[1,128,128]{1,2,0:T(8,128)S(1)}, f32[1,128,128]{1,2,0:T(8,128)S(1)}, u32[]{:S(2)}, u32[]{:S(2)}) collective-permute-start(f32[1,128,128]{1,2,0:T(8,128)S(1)} %get-tuple-element.507), channel_id=1, source_target_pairs={{4,0},{8,4},{12,8},{16,12},{20,16},{24,20},{28,24},{5,1},{9,5},{13... | collective-permute-start | bytes 196616 | tf_op jit(solution)/shard_map/ppermute | solution.py:15
  16.4 330.1 %collective-permute-start.7 = (f32[1,128,128]{1,2,0:T(8,128)S(1)}, f32[1,128,128]{1,2,0:T(8,128)S(1)}, u32[]{:S(2)}, u32[]{:S(2)}) collective-permute-start(f32[1,128,128]{1,2,0:T(8,128)S(1)} %get-tuple-element.506), channel_id=1, source_target_pairs={{0,4},{4,8},{8,12},{12,16},{16,20},{20,24},{24,28},{1,5},{5,9},{9,... | collective-permute-start | bytes 196616 | tf_op jit(solution)/shard_map/ppermute | solution.py:14
  59.0 3.3 collective-permute-start.1
  63.1 17.3 %collective-permute-start.1 = (f32[512,32]{0,1:T(8,128)S(1)}, f32[512,32]{0,1:T(8,128)S(1)}, u32[]{:S(2)}, u32[]{:S(2)}) collective-permute-start(f32[512,32]{0,1:T(8,128)S(1)} %get-tuple-element.643), channel_id=1, source_target_pairs={{0,4},{4,8},{8,12},{12,16},{16,20},{20,24},{24,28},{1,5},{5,9},{9,... | collective-permute-start | bytes 196616 | tf_op jit(solution)/shard_map/while/body/eval_jaxpr/ppermute | solution.py:23
  81.1 6.1 %collective-permute-start.1 = (f32[512,32]{0,1:T(8,128)S(1)}, f32[512,32]{0,1:T(8,128)S(1)}, u32[]{:S(2)}, u32[]{:S(2)}) collective-permute-start(f32[512,32]{0,1:T(8,128)S(1)} %get-tuple-element.643), channel_id=1, source_target_pairs={{0,4},{4,8},{8,12},{12,16},{16,20},{20,24},{24,28},{1,5},{5,9},{9,... | collective-permute-start | bytes 196616 | tf_op jit(solution)/shard_map/while/body/eval_jaxpr/ppermute | solution.py:23
  87.9 15.7 %collective-permute-start.1 = (f32[512,32]{0,1:T(8,128)S(1)}, f32[512,32]{0,1:T(8,128)S(1)}, u32[]{:S(2)}, u32[]{:S(2)}) collective-permute-start(f32[512,32]{0,1:T(8,128)S(1)} %get-tuple-element.643), channel_id=1, source_target_pairs={{0,4},{4,8},{8,12},{12,16},{16,20},{20,24},{24,28},{1,5},{5,9},{9,... | collective-permute-start | bytes 196616 | tf_op jit(solution)/shard_map/while/body/eval_jaxpr/ppermute | solution.py:23
  104.4 7.0 %collective-permute-start.1 = (f32[512,32]{0,1:T(8,128)S(1)}, f32[512,32]{0,1:T(8,128)S(1)}, u32[]{:S(2)}, u32[]{:S(2)}) collective-permute-start(f32[512,32]{0,1:T(8,128)S(1)} %get-tuple-element.643), channel_id=1, source_target_pairs={{0,4},{4,8},{8,12},{12,16},{16,20},{20,24},{24,28},{1,5},{5,9},{9,... | collective-permute-start | bytes 196616 | tf_op jit(solution)/shard_map/while/body/eval_jaxpr/ppermute | solution.py:23
  112.1 13.9 %collective-permute-start.1 = (f32[512,32]{0,1:T(8,128)S(1)}, f32[512,32]{0,1:T(8,128)S(1)}, u32[]{:S(2)}, u32[]{:S(2)}) collective-permute-start(f32[512,32]{0,1:T(8,128)S(1)} %get-tuple-element.643), channel_id=1, source_target_pairs={{0,4},{4,8},{8,12},{12,16},{16,20},{20,24},{24,28},{1,5},{5,9},{9,... | collective-permute-start | bytes 196616 | tf_op jit(solution)/shard_map/while/body/eval_jaxpr/ppermute | solution.py:23
  126.8 7.0 %collective-permute-start.1 = (f32[512,32]{0,1:T(8,128)S(1)}, f32[512,32]{0,1:T(8,128)S(1)}, u32[]{:S(2)}, u32[]{:S(2)}) collective-permute-start(f32[512,32]{0,1:T(8,128)S(1)} %get-tuple-element.643), channel_id=1, source_target_pairs={{0,4},{4,8},{8,12},{12,16},{16,20},{20,24},{24,28},{1,5},{5,9},{9,... | collective-permute-start | bytes 196616 | tf_op jit(solution)/shard_map/while/body/eval_jaxpr/ppermute | solution.py:23
  134.6 14.8 %collective-permute-start.1 = (f32[512,32]{0,1:T(8,128)S(1)}, f32[512,32]{0,1:T(8,128)S(1)}, u32[]{:S(2)}, u32[]{:S(2)}) collective-permute-start(f32[512,32]{0,1:T(8,128)S(1)} %get-tuple-element.643), channel_id=1, source_target_pairs={{0,4},{4,8},{8,12},{12,16},{16,20},{20,24},{24,28},{1,5},{5,9},{9,... | collective-permute-start | bytes 196616 | tf_op jit(solution)/shard_map/while/body/eval_jaxpr/ppermute | solution.py:23
  150.1 7.4 %collective-permute-start = (f32[512,32]{0,1:T(8,128)S(1)}, f32[512,32]{0,1:T(8,128)S(1)}, u32[]{:S(2)}, u32[]{:S(2)}) collective-permute-start(f32[512,32]{0,1:T(8,128)S(1)} %get-tuple-element.651), channel_id=1, source_target_pairs={{4,0},{8,4},{12,8},{16,12},{20,16},{24,20},{28,24},{5,1},{9,5},{13... | collective-permute-start | bytes 196616 | tf_op jit(solution)/shard_map/while/body/eval_jaxpr/ppermute | solution.py:23
  158.2 14.9 %collective-permute-start = (f32[512,32]{0,1:T(8,128)S(1)}, f32[512,32]{0,1:T(8,128)S(1)}, u32[]{:S(2)}, u32[]{:S(2)}) collective-permute-start(f32[512,32]{0,1:T(8,128)S(1)} %get-tuple-element.651), channel_id=1, source_target_pairs={{4,0},{8,4},{12,8},{16,12},{20,16},{24,20},{28,24},{5,1},{9,5},{13... | collective-permute-start | bytes 196616 | tf_op jit(solution)/shard_map/while/body/eval_jaxpr/ppermute | solution.py:23
  173.8 7.0 %collective-permute-start = (f32[512,32]{0,1:T(8,128)S(1)}, f32[512,32]{0,1:T(8,128)S(1)}, u32[]{:S(2)}, u32[]{:S(2)}) collective-permute-start(f32[512,32]{0,1:T(8,128)S(1)} %get-tuple-element.651), channel_id=1, source_target_pairs={{4,0},{8,4},{12,8},{16,12},{20,16},{24,20},{28,24},{5,1},{9,5},{13... | collective-permute-start | bytes 196616 | tf_op jit(solution)/shard_map/while/body/eval_jaxpr/ppermute | solution.py:23
  181.6 15.5 %collective-permute-start = (f32[512,32]{0,1:T(8,128)S(1)}, f32[512,32]{0,1:T(8,128)S(1)}, u32[]{:S(2)}, u32[]{:S(2)}) collective-permute-start(f32[512,32]{0,1:T(8,128)S(1)} %get-tuple-element.651), channel_id=1, source_target_pairs={{4,0},{8,4},{12,8},{16,12},{20,16},{24,20},{28,24},{5,1},{9,5},{13... | collective-permute-start | bytes 196616 | tf_op jit(solution)/shard_map/while/body/eval_jaxpr/ppermute | solution.py:23
  197.8 7.0 %collective-permute-start = (f32[512,32]{0,1:T(8,128)S(1)}, f32[512,32]{0,1:T(8,128)S(1)}, u32[]{:S(2)}, u32[]{:S(2)}) collective-permute-start(f32[512,32]{0,1:T(8,128)S(1)} %get-tuple-element.651), channel_id=1, source_target_pairs={{4,0},{8,4},{12,8},{16,12},{20,16},{24,20},{28,24},{5,1},{9,5},{13... | collective-permute-start | bytes 196616 | tf_op jit(solution)/shard_map/while/body/eval_jaxpr/ppermute | solution.py:23
  205.6 14.0 %collective-permute-start = (f32[512,32]{0,1:T(8,128)S(1)}, f32[512,32]{0,1:T(8,128)S(1)}, u32[]{:S(2)}, u32[]{:S(2)}) collective-permute-start(f32[512,32]{0,1:T(8,128)S(1)} %get-tuple-element.651), channel_id=1, source_target_pairs={{4,0},{8,4},{12,8},{16,12},{20,16},{24,20},{28,24},{5,1},{9,5},{13... | collective-permute-start | bytes 196616 | tf_op jit(solution)/shard_map/while/body/eval_jaxpr/ppermute | solution.py:23
  220.3 87.8 %collective-permute-start = (f32[512,32]{0,1:T(8,128)S(1)}, f32[512,32]{0,1:T(8,128)S(1)}, u32[]{:S(2)}, u32[]{:S(2)}) collective-permute-start(f32[512,32]{0,1:T(8,128)S(1)} %get-tuple-element.651), channel_id=1, source_target_pairs={{4,0},{8,4},{12,8},{16,12},{20,16},{24,20},{28,24},{5,1},{9,5},{13... | collective-permute-start | bytes 196616 | tf_op jit(solution)/shard_map/while/body/eval_jaxpr/ppermute | solution.py:23
  320.5 6.2 %collective-permute-start = (f32[512,32]{0,1:T(8,128)S(1)}, f32[512,32]{0,1:T(8,128)S(1)}, u32[]{:S(2)}, u32[]{:S(2)}) collective-permute-start(f32[512,32]{0,1:T(8,128)S(1)} %get-tuple-element.651), channel_id=1, source_target_pairs={{4,0},{8,4},{12,8},{16,12},{20,16},{24,20},{28,24},{5,1},{9,5},{13... | collective-permute-start | bytes 196616 | tf_op jit(solution)/shard_map/while/body/eval_jaxpr/ppermute | solution.py:23
  328.4 9.4 %all-to-all-start.1 = ((f32[4,1,16384]{2,1,0:T(1,128)}), f32[4,1,16384]{2,1,0:T(1,128)S(1)}, u32[]{:S(2)}, u32[]{:S(2)}) async-start(f32[4,1,16384]{2,1,0:T(1,128)} %reshape.6), calls=%async_computation.1 | async-start | bytes 524288 | tf_op jit(solution)/shard_map/all_to_all | solution.py:103
  340.6 6.3 %collective-permute-start.2 = (f32[1,128,128]{1,2,0:T(8,128)S(1)}, f32[1,128,128]{1,2,0:T(8,128)S(1)}, u32[]{:S(2)}, u32[]{:S(2)}) collective-permute-start(f32[1,128,128]{1,2,0:T(8,128)S(1)} %bitcast.60), channel_id=1, source_target_pairs={{4,0},{8,4},{12,8},{16,12},{20,16},{24,20},{28,24},{5,1},{9,5},{13... | collective-permute-start | bytes 196616 | tf_op jit(solution)/shard_map/ppermute | solution.py:15
  341.9 6.4 %collective-permute-start.3 = (f32[1,128,128]{1,2,0:T(8,128)S(1)}, f32[1,128,128]{1,2,0:T(8,128)S(1)}, u32[]{:S(2)}, u32[]{:S(2)}) collective-permute-start(f32[1,128,128]{1,2,0:T(8,128)S(1)} %bitcast.61), channel_id=1, source_target_pairs={{0,4},{4,8},{8,12},{12,16},{16,20},{20,24},{24,28},{1,5},{5,9},{9,... | collective-permute-start | bytes 196616 | tf_op jit(solution)/shard_map/ppermute | solution.py:14
  348.6 4.4 %collective-permute-start.4 = (f32[6,1,128]{1,2,0:T(8,128)S(1)}, f32[6,1,128]{1,2,0:T(8,128)S(1)}, u32[]{:S(2)}, u32[]{:S(2)}) collective-permute-start(f32[6,1,128]{1,2,0:T(8,128)S(1)} %get-tuple-element.500), channel_id=1, source_target_pairs={{1,0},{2,1},{3,2},{5,4},{6,5},{7,6},{9,8},{10,9},{11,10},{13,12},{... | collective-permute-start | bytes 9224 | tf_op jit(solution)/shard_map/ppermute | solution.py:15
  349.9 4.4 collective-permute-start.5
  354.6 13.4 %collective-permute-start.10 = (f32[1,128,128]{1,2,0:T(8,128)S(1)}, f32[1,128,128]{1,2,0:T(8,128)S(1)}, u32[]{:S(2)}, u32[]{:S(2)}) collective-permute-start(f32[1,128,128]{1,2,0:T(8,128)S(1)} %get-tuple-element.503), channel_id=1, source_target_pairs={{4,0},{8,4},{12,8},{16,12},{20,16},{24,20},{28,24},{5,1},{9,5},{13... | collective-permute-start | bytes 196616 | tf_op jit(solution)/shard_map/ppermute | solution.py:15
  355.9 12.1 %collective-permute-start.11 = (f32[1,128,128]{1,2,0:T(8,128)S(1)}, f32[1,128,128]{1,2,0:T(8,128)S(1)}, u32[]{:S(2)}, u32[]{:S(2)}) collective-permute-start(f32[1,128,128]{1,2,0:T(8,128)S(1)} %get-tuple-element.502), channel_id=1, source_target_pairs={{0,4},{4,8},{8,12},{12,16},{16,20},{20,24},{24,28},{1,5},{5,9},{9,... | collective-permute-start | bytes 196616 | tf_op jit(solution)/shard_map/ppermute | solution.py:14
  360.9 13.9 %collective-permute-start.8 = (f32[6,1,128]{1,2,0:T(8,128)S(1)}, f32[6,1,128]{1,2,0:T(8,128)S(1)}, u32[]{:S(2)}, u32[]{:S(2)}) collective-permute-start(f32[6,1,128]{1,2,0:T(8,128)S(1)} %get-tuple-element.498), channel_id=1, source_target_pairs={{1,0},{2,1},{3,2},{5,4},{6,5},{7,6},{9,8},{10,9},{11,10},{13,12},{... | collective-permute-start | bytes 9224 | tf_op jit(solution)/shard_map/ppermute | solution.py:15
  362.2 12.6 %collective-permute-start.9 = (f32[6,1,128]{1,2,0:T(8,128)S(1)}, f32[6,1,128]{1,2,0:T(8,128)S(1)}, u32[]{:S(2)}, u32[]{:S(2)}) collective-permute-start(f32[6,1,128]{1,2,0:T(8,128)S(1)} %get-tuple-element.499), channel_id=1, source_target_pairs={{0,1},{1,2},{2,3},{4,5},{5,6},{6,7},{8,9},{9,10},{10,11},{12,13},{... | collective-permute-start | bytes 9224 | tf_op jit(solution)/shard_map/ppermute | solution.py:14
  368.2 6.7 %collective-permute-start.12 = (f32[6,1,128]{1,2,0:T(8,128)S(1)}, f32[6,1,128]{1,2,0:T(8,128)S(1)}, u32[]{:S(2)}, u32[]{:S(2)}) collective-permute-start(f32[6,1,128]{1,2,0:T(8,128)S(1)} %get-tuple-element.496), channel_id=1, source_target_pairs={{1,0},{2,1},{3,2},{5,4},{6,5},{7,6},{9,8},{10,9},{11,10},{13,12},{... | collective-permute-start | bytes 9224 | tf_op jit(solution)/shard_map/ppermute | solution.py:15
  369.5 6.6 %collective-permute-start.13 = (f32[6,1,128]{1,2,0:T(8,128)S(1)}, f32[6,1,128]{1,2,0:T(8,128)S(1)}, u32[]{:S(2)}, u32[]{:S(2)}) collective-permute-start(f32[6,1,128]{1,2,0:T(8,128)S(1)} %get-tuple-element.497), channel_id=1, source_target_pairs={{0,1},{1,2},{2,3},{4,5},{5,6},{6,7},{8,9},{9,10},{10,11},{12,13},{... | collective-permute-start | bytes 9224 | tf_op jit(solution)/shard_map/ppermute | solution.py:14
Sparse Core Ops, SparseCore 0:
  9.5 37.7 all-gather.1
where the time goes:
time: 441 us; the launch traced here: 438 us
  waiting for transfers between devices  195 us (44%)
  starting transfers between devices  124 us (28%)
  blocking collectives  45.9 us (10%)
  matrix products  23.3 us (5%)
  local copies, waits for them, and re-layouts  21 us (5%)
  between operations  20.8 us (5%)
  other arithmetic  8.15 us (2%)
    ppermute x16, waiting for transfers between devices, from_behind(): return lax.ppermute(block, axis, route)  161 us
    ppermute x16, starting transfers between devices, from_behind(): return lax.ppermute(block, axis, route)  80.1 us
    psum x1, blocking collectives, per_device(): lax.psum((jnp.sum(right_side * right_side), jnp.sum(right_side * image),...  45.9 us
    ppermute x6, starting transfers between devices, with_halo(): before = lax.ppermute(last, axis, up)  28.1 us
    all_gather x1, waiting for transfers between devices, per_device(): matrices = lax.all_gather(inverses, 'split', axis=2, tiled=True)  23.4 us
    dot_general x4, matrix products, down_advance(): state = jnp.dot(matrix, source + state, precision=lax.Precision.HIGHEST)  11.7 us
    dot_general x4, matrix products, up_advance(): state = below + jnp.dot(matrix, state, precision=lax.Precision.HIGHEST)  11.7 us
    another operation x31, local copies, waits for them, and re-layouts  11 us
  transfers between devices with their start and end apart: 31, of which 21 were waited for; matrix products, arithmetic and copies ran while one was open for 11% of the time, Pallas kernels for 0%

commit v1 on v0

v1 whole, which is shorter than its diff:
```python
import functools

import jax
import jax.numpy as jnp
from jax import lax
from jax.experimental import pallas as pl
from jax.experimental.pallas import tpu as pltpu
from jax.sharding import PartitionSpec as P

MESH = pl.DeviceIdType.MESH
F32, BF16 = jnp.float32, jnp.bfloat16


def halves(a):
    hi = a.astype(BF16)
    return hi, (a - hi.astype(F32)).astype(BF16)


def product(a_hi, a_lo, b_hi, b_lo, axis):
    dims = (((1,), (axis,)), ((), ()))

    def one(a, b):
        return lax.dot_general(a, b, dims, preferred_element_type=F32)

    return one(a_hi, b_hi) + (one(a_lo, b_hi) + one(a_hi, b_lo))


def sweep_kernel(
    depth, parts, rs_ref, inv_ref, out_ref,
    mf, mhi, mlo, whi, wlo, uhi, ulo, loc, base, rsend, rrecv, vin, vout, din, dout, dsend, drecv,
    own_sem, gs_sem, gr_sem, as_sem, ar_sem, bs_sem, br_sem, vs_sem, vr_sem, ds_sem, dr_sem,
):
    planes, nx, xb = inv_ref.shape
    ny = rs_ref.shape[2]
    yb = ny // parts
    chunks = vin.shape[0]
    cb = yb // chunks
    l, s = lax.axis_index("layer"), lax.axis_index("split")
    bits = [1 << i for i in range(parts.bit_length() - 1)]

    barrier = pltpu.get_barrier_semaphore()
    for r in range(1, parts):
        pl.semaphore_signal(barrier, inc=1, device_id=(l, s ^ r), device_id_type=MESH)
    pl.semaphore_signal(barrier, inc=1, device_id=(lax.rem(l + 1, depth), s), device_id_type=MESH)
    pl.semaphore_signal(barrier, inc=1, device_id=(lax.rem(l + depth - 1, depth), s), device_id_type=MESH)

    def own_copy(k):
        return pltpu.make_async_copy(inv_ref.at[k], mf.at[k, s], own_sem.at[k])

    for k in range(planes):
        own_copy(k).start()
    for k in range(planes):
        turned = jnp.transpose(rs_ref[k])
        for r in range(parts):
            rsend[r, k] = turned[r * yb:(r + 1) * yb]
    pl.semaphore_wait(barrier, parts + 1)

    def regroup(src, dst, ssem, rsem, r):
        return pltpu.make_async_remote_copy(
            src_ref=src.at[s ^ r], dst_ref=dst.at[s], send_sem=ssem.at[r], recv_sem=rsem.at[r],
            device_id=(l, s ^ r), device_id_type=MESH)

    def regroup_in(src, dst, ssem, rsem, r):
        return pltpu.make_async_remote_copy(
            src_ref=src.at[s ^ r], dst_ref=dst.at[s ^ r], send_sem=ssem.at[r], recv_sem=rsem.at[r],
            device_id=(l, s ^ r), device_id_type=MESH)

    def shift(k, r, b):
        src = inv_ref.at[k] if r == 0 else mf.at[k, s ^ r]
        return pltpu.make_async_remote_copy(
            src_ref=src, dst_ref=mf.at[k, s ^ r], send_sem=gs_sem.at[k, r ^ b], recv_sem=gr_sem.at[k, r ^ b],
            device_id=(l, s ^ b), device_id_type=MESH)

    def arrived(k, r):
        return pltpu.make_async_remote_copy(
            src_ref=mf.at[k, s ^ r], dst_ref=mf.at[k, s ^ r], send_sem=gs_sem.at[k, r], recv_sem=gr_sem.at[k, r],
            device_id=(l, s ^ 1), device_id_type=MESH)

    for r in range(1, parts):
        regroup(rsend, rrecv, as_sem, ar_sem, r).start()
    for k in range(planes):
        for b in reversed(bits):
            shift(k, 0, b).start()
    rrecv[s] = rsend[s]
    for r in range(1, parts):
        regroup_in(rsend, rrecv, as_sem, ar_sem, r).wait_recv()

    def fetch(k):
        for r in range(1, parts):
            arrived(k, r).wait_recv()
            for b in bits:
                if b < (r & -r):
                    shift(k, r, b).start()
        own_copy(k).wait()
        for j in range(parts):
            hi, lo = halves(mf[k, j])
            mhi[k, :, j * xb:(j + 1) * xb] = hi
            mlo[k, :, j * xb:(j + 1) * xb] = lo

    def source(k):
        return jnp.concatenate([rrecv[j, k] for j in range(parts)], axis=1)

    half = nx // 2

    fetch(0)
    for j in range(parts):
        hi, lo = halves(jnp.transpose(mf[0, j]))
        whi[0, j * xb:(j + 1) * xb] = hi
        wlo[0, j * xb:(j + 1) * xb] = lo
    loc[0] = product(*halves(source(0)), mhi[0], mlo[0], 1)

    @pl.loop(1, planes)
    def _(k):
        fetch(k)
        loc[k] = product(*halves(source(k) + loc[k - 1]), mhi[k], mlo[k], 1)
        for t in range(2):
            rows = slice(t * half, (t + 1) * half)
            hi, lo = halves(product(whi[k - 1, rows], wlo[k - 1, rows], mhi[k], mlo[k], 1))
            whi[k, rows] = hi
            wlo[k, rows] = lo

    last = planes - 1

    def hop(src, dst, ssem, rsem, c, step):
        return pltpu.make_async_remote_copy(
            src_ref=src.at[c], dst_ref=dst.at[c], send_sem=ssem.at[c], recv_sem=rsem.at[c],
            device_id=(lax.rem(l + step + depth, depth), s), device_id_type=MESH)

    def down_chain():
        for c in range(chunks):
            rows = slice(c * cb, (c + 1) * cb)

            @pl.when(l > 0)
            def _():
                hop(vout, vin, vs_sem, vr_sem, c, 1).wait_recv()

            @pl.when(l == 0)
            def _():
                vin[c] = jnp.zeros_like(vin[c])

            vout[c] = loc[last, rows] + product(*halves(vin[c]), whi[last], wlo[last], 0)

            @pl.when(l < depth - 1)
            def _():
                hop(vout, vin, vs_sem, vr_sem, c, 1).start()

    def compose():
        for j in range(parts):
            hi, lo = halves(jnp.transpose(mf[last, j]))
            uhi[last, j * xb:(j + 1) * xb] = hi
            ulo[last, j * xb:(j + 1) * xb] = lo

        @pl.loop(0, last)
        def _(i):
            k = last - 1 - i
            loc[k] = loc[k] + product(*halves(loc[k + 1]), mhi[k], mlo[k], 1)
            for t in range(2):
                rows = slice(t * half, (t + 1) * half)
                hi, lo = halves(product(uhi[k + 1, rows], ulo[k + 1, rows], mhi[k], mlo[k], 1))
                uhi[k, rows] = hi
                ulo[k, rows] = lo
                own = whi[k, rows].astype(F32) + wlo[k, rows].astype(F32)
                hi, lo = halves(own + product(whi[k + 1, rows], wlo[k + 1, rows], mhi[k], mlo[k], 1))
                whi[k, rows] = hi
                wlo[k, rows] = lo

    early = lax.convert_element_type(l < depth // 2, jnp.int32)

    @pl.loop(0, 2)
    def _(turn):
        @pl.when(turn != early)
        def _():
            down_chain()

        @pl.when(turn == early)
        def _():
            compose()

    entering = jnp.concatenate([vin[c] for c in range(chunks)], axis=0)
    entering = halves(entering)

    @pl.loop(0, planes)
    def _(k):
        base[k] = loc[k] + product(*entering, whi[k], wlo[k], 0)

    for c in range(chunks):
        rows = slice(c * cb, (c + 1) * cb)

        @pl.when(l < depth - 1)
        def _():
            hop(dout, din, ds_sem, dr_sem, c, -1).wait_recv()

        @pl.when(l == depth - 1)
        def _():
            din[c] = jnp.zeros_like(din[c])

        dout[c] = base[0, rows] + product(*halves(din[c]), uhi[0], ulo[0], 0)

        @pl.when(l > 0)
        def _():
            hop(dout, din, ds_sem, dr_sem, c, -1).start()

    entering = halves(jnp.concatenate([din[c] for c in range(chunks)], axis=0))

    @pl.loop(0, planes)
    def _(k):
        swept = base[k] + product(*entering, uhi[k], ulo[k], 0)
        for j in range(parts):
            dsend[j, k] = swept[:, j * xb:(j + 1) * xb]

    for r in range(1, parts):
        regroup(dsend, drecv, bs_sem, br_sem, r).start()
    drecv[s] = dsend[s]
    for r in range(1, parts):
        regroup_in(dsend, drecv, bs_sem, br_sem, r).wait_recv()
    for k in range(planes):
        out_ref[k] = jnp.transpose(jnp.concatenate([drecv[j, k] for j in range(parts)], axis=0))

    for r in range(1, parts):
        regroup(rsend, rrecv, as_sem, ar_sem, r).wait_send()
        regroup(dsend, drecv, bs_sem, br_sem, r).wait_send()
    for k in range(planes):
        for r in range(1, parts):
            arrived(k, r).wait_send()
    for c in range(chunks):
        @pl.when(l < depth - 1)
        def _():
            hop(vout, vin, vs_sem, vr_sem, c, 1).wait_send()

        @pl.when(l > 0)
        def _():
            hop(dout, din, ds_sem, dr_sem, c, -1).wait_send()


def sweep(right_side, inverses):
    depth, parts = lax.axis_size("layer"), lax.axis_size("split")
    planes, nx, xb = inverses.shape
    ny = right_side.shape[2]
    yb = ny // parts
    chunks = 2 if yb % 16 == 0 else 1
    square = pltpu.VMEM((planes, nx, nx), BF16)
    lines = pltpu.VMEM((planes, yb, nx), F32)
    pieces = pltpu.VMEM((parts, planes, yb, xb), F32)
    carry = pltpu.VMEM((chunks, yb // chunks, nx), F32)
    dma = pltpu.SemaphoreType.DMA
    return pl.pallas_call(
        functools.partial(sweep_kernel, depth, parts),
        out_shape=jax.ShapeDtypeStruct(right_side.shape, F32),
        in_specs=[pl.BlockSpec(memory_space=pltpu.VMEM)] * 2,
        out_specs=pl.BlockSpec(memory_space=pltpu.VMEM),
        scratch_shapes=[
            pltpu.VMEM((planes, parts, nx, xb), F32),
            square, square, square, square, square, square,
            lines, lines, pieces, pieces, carry, carry, carry, carry, pieces, pieces,
            dma((planes,)), dma((planes, parts)), dma((planes, parts)),
            dma((parts,)), dma((parts,)), dma((parts,)), dma((parts,)),
            dma((chunks,)), dma((chunks,)), dma((chunks,)), dma((chunks,)),
        ],
        compiler_params=pltpu.CompilerParams(
            collective_id=0, has_side_effects=True, vmem_limit_bytes=60 * 1024 * 1024),
    )(right_side, inverses)


def with_halo(x, sides, width):
    for axis, dim in sides:
        size, length = (lax.axis_size(axis), x.shape[dim])
        up = [(i, (i + 1) % size) for i in range(size - 1)]
        down = [(j, i) for i, j in up]
        last = lax.slice_in_dim(x, length - width, length, axis=dim)
        first = lax.slice_in_dim(x, 0, width, axis=dim)
        before = lax.ppermute(last, axis, up)
        after = lax.ppermute(first, axis, down)
        x = jnp.concatenate([before, x, after], axis=dim)
    return x


def stencil(values, diagonal):
    padded = with_halo(values, (("layer", 0), ("split", 1)), 1)
    beside = padded[2:, 1:-1, :] + padded[:-2, 1:-1, :]
    beside = beside + padded[1:-1, 2:, :] + padded[1:-1, :-2, :]
    centre_part = padded[1:-1, 1:-1, :]
    y_upper = jnp.pad(centre_part[:, :, 1:], ((0, 0), (0, 0), (0, 1)))
    y_lower = jnp.pad(centre_part[:, :, :-1], ((0, 0), (0, 0), (1, 0)))
    return (6.0 + diagonal) * values - beside - y_upper - y_lower


def per_device(right_side, diagonal, inverses):
    applied_rhs = stencil(right_side, diagonal)
    direction = sweep(right_side, inverses)
    image = stencil(direction, diagonal)
    applied_image = stencil(image, diagonal)
    sums_all = lax.psum(
        (
            jnp.sum(right_side * right_side),
            jnp.sum(right_side * image),
            jnp.sum(applied_rhs * right_side),
            jnp.sum(applied_rhs * image),
            jnp.sum(applied_image * right_side),
            jnp.sum(applied_image * image),
            jnp.sum(applied_rhs * applied_rhs),
            jnp.sum(applied_rhs * applied_image),
            jnp.sum(applied_image * applied_image),
        ),
        ("layer", "split"),
    )
    (
        norm_sq,
        curv_sum,
        rhs_rhs,
        rhs_image,
        image_rhs,
        image_image,
        arhs_arhs,
        arhs_aimage,
        aimage_aimage,
    ) = sums_all
    step_alpha = norm_sq / curv_sum
    middle = right_side - step_alpha * image
    tangent = applied_rhs - step_alpha * applied_image
    cross_sum = (
        rhs_rhs - step_alpha * (rhs_image + image_rhs) + step_alpha * step_alpha * image_image
    )
    self_sum = arhs_arhs - 2.0 * step_alpha * arhs_aimage + step_alpha * step_alpha * aimage_aimage
    step_omega = cross_sum / self_sum
    solution_field = step_alpha * direction + step_omega * middle
    residual = middle - step_omega * tangent
    return (solution_field, residual)


def solution(mesh):
    placed = (P("layer", "split", None), P("layer", "split", None), P("layer", None, "split"))
    return jax.shard_map(
        per_device,
        mesh=mesh,
        in_specs=placed,
        out_specs=(P("layer", "split", None), P("layer", "split", None)),
        check_vma=False,
    )
```

time: 441 us -> 178 us (0.40)
  waiting for transfers between devices: 195 us -> 6.1 us
  starting transfers between devices: 124 us -> 26.8 us
  Pallas kernels: 0 us -> 89.7 us
  matrix products: 23.3 us -> 0 us
  local copies, waits for them, and re-layouts: 21 us -> 3.24 us
  between operations: 20.8 us -> 7.19 us
  other arithmetic: 8.15 us -> 2.13 us
    ppermute x16 -> x0, waiting for transfers between devices: 161 us -> none  [from_behind(): return lax.ppermute(block, axis, route)]
    pallas_call x0 -> x1, Pallas kernels: none -> 89.7 us  [sweep(): pl.pallas_call(functools.partial(sweep_kernel, depth, parts), out_shape=j...]
    ppermute x16 -> x0, starting transfers between devices: 80.1 us -> none  [from_behind(): return lax.ppermute(block, axis, route)]
    all_gather x1 -> x0, waiting for transfers between devices: 23.4 us -> none  [per_device(): matrices = lax.all_gather(inverses, 'split', axis=2, tiled=True)]
    dot_general x8 -> x0, matrix products: 23.3 us -> none  [the longest x4 11.7 us: down_advance(): state = jnp.dot(matrix, source + state, precision=lax.Precision.HIGHEST)]
    another operation x31 -> x0, local copies, waits for them, and re-layouts: 11 us -> none
    ppermute x6, starting transfers between devices: 28.1 us -> 19.1 us  [with_halo(): before = lax.ppermute(last, axis, up)]
    all_to_all x2 -> x0, starting transfers between devices: 7.67 us -> none  [the longest x1 4.26 us: per_device(): lax.all_to_all(right_side, 'split', split_axis=2, concat_axis=1, tiled=True)]
  transfers between devices with their start and end apart: 31 -> 12, of which waited for: 21 -> 5; matrix products, arithmetic and copies ran while one was open for 11% -> 1% of each run, Pallas kernels for 0% -> 51%
where the time goes in v1:
time: 178 us; the launch traced here: 177 us
  Pallas kernels  89.7 us (50%)
  blocking collectives  42.2 us (24%)
  starting transfers between devices  26.8 us (15%)
  between operations  7.19 us (4%)
  waiting for transfers between devices  6.1 us (3%)
  local copies, waits for them, and re-layouts  3.24 us (2%)
  other arithmetic  2.13 us (1%)
    pallas_call x1, Pallas kernels, sweep(): pl.pallas_call(functools.partial(sweep_kernel, depth, parts), out_shape=j...  89.7 us
    psum x1, blocking collectives, per_device(): lax.psum((jnp.sum(right_side * right_side), jnp.sum(right_side * image),...  42.2 us
    ppermute x6, starting transfers between devices, with_halo(): before = lax.ppermute(last, axis, up)  19.1 us
    ppermute x6, starting transfers between devices, with_halo(): after = lax.ppermute(first, axis, down)  7.73 us
  transfers between devices with their start and end apart: 12, of which 5 were waited for; matrix products, arithmetic and copies ran while one was open for 1% of the time, Pallas kernels for 51%

profile of v1, /device:TPU:0, one launch (start us, length us, event | category | flops | bytes accessed | tf_op | source)
XLA Modules:
  0.0 177.4 jit_solution(15716149546891220326)
XLA Ops:
  0.6 0.9 fusion.23
  1.5 1.3 collective-permute-start.4
  2.8 5.5 %collective-permute-start.5 = (f32[1,128,128]{2,1,0:T(8,128)S(1)}, f32[1,128,128]{2,1,0:T(8,128)S(1)}, u32[]{:S(2)}, u32[]{:S(2)}) collective-permute-start(f32[1,128,128]{2,1,0:T(8,128)S(1)} %get-tuple-element.34), channel_id=1, source_target_pairs={{0,4},{4,8},{8,12},{12,16},{16,20},{20,24},{24,28},{1,5},{5,9},{9,... | collective-permute-start | bytes 196616 | tf_op jit(solution)/shard_map/ppermute | solution.py:271
  8.3 89.7 %shard_map.50 = f32[4,128,128]{2,1,0:T(8,128)} custom-call(f32[4,128,128]{2,1,0:T(8,128)} %rs_ref.1, f32[4,512,128]{2,1,0:T(8,128)} %inv_ref.1), custom_call_target="tpu_custom_call" | custom-call | tf_op jit(solution)/shard_map/pallas_call | solution.py:246
  98.1 0.9 fusion.26
  99.0 1.3 collective-permute-start.1
  100.3 1.3 collective-permute-start
  101.6 0.0 copy-start
  101.6 0.1 fusion.25
  101.7 0.8 copy-done
  102.6 0.1 fusion.24
  102.7 1.3 collective-permute-done.1
  104.0 2.7 %collective-permute-done = f32[1,128,128]{2,1,0:T(8,128)S(1)} collective-permute-done((f32[1,128,128]{2,1,0:T(8,128)S(1)}, f32[1,128,128]{2,1,0:T(8,128)S(1)}, u32[]{:S(2)}, u32[]{:S(2)}) %collective-permute-start) | collective-permute-done | bytes 65568 | tf_op jit(solution)/shard_map/ppermute | solution.py:272
  106.7 1.3 collective-permute-start.2
  108.0 3.0 %collective-permute-start.3 = (f32[6,1,128]{2,1,0:T(1,128)S(1)}, f32[6,1,128]{2,1,0:T(1,128)S(1)}, u32[]{:S(2)}, u32[]{:S(2)}) collective-permute-start(f32[6,1,128]{2,1,0:T(1,128)S(1)} %get-tuple-element.28), channel_id=1, source_target_pairs={{0,1},{1,2},{2,3},{4,5},{5,6},{6,7},{8,9},{9,10},{10,11},{12,13},{... | collective-permute-start | bytes 9224 | tf_op jit(solution)/shard_map/ppermute | solution.py:271
  111.0 0.0 collective-permute-done.5
  111.1 0.0 copy-start.2
  111.1 0.7 collective-permute-done.3
  111.8 0.2 copy-done.2
  112.0 0.1 fusion.15
  112.2 1.7 collective-permute-start.9
  113.9 1.3 collective-permute-start.8
  115.2 1.3 collective-permute-start.6
  116.5 3.4 %collective-permute-start.7 = (f32[6,1,128]{2,1,0:T(1,128)S(1)}, f32[6,1,128]{2,1,0:T(1,128)S(1)}, u32[]{:S(2)}, u32[]{:S(2)}) collective-permute-start(f32[6,1,128]{2,1,0:T(1,128)S(1)} %get-tuple-element.26), channel_id=1, source_target_pairs={{0,1},{1,2},{2,3},{4,5},{5,6},{6,7},{8,9},{9,10},{10,11},{12,13},{... | collective-permute-start | bytes 9224 | tf_op jit(solution)/shard_map/ppermute | solution.py:271
  120.0 0.7 collective-permute-done.8
  120.7 1.3 collective-permute-start.10
  122.0 4.1 %collective-permute-start.11 = (f32[6,1,128]{2,1,0:T(1,128)S(1)}, f32[6,1,128]{2,1,0:T(1,128)S(1)}, u32[]{:S(2)}, u32[]{:S(2)}) collective-permute-start(f32[6,1,128]{2,1,0:T(1,128)S(1)} %get-tuple-element.24), channel_id=1, source_target_pairs={{0,1},{1,2},{2,3},{4,5},{5,6},{6,7},{8,9},{9,10},{10,11},{12,13},{... | collective-permute-start | bytes 9224 | tf_op jit(solution)/shard_map/ppermute | solution.py:271
  126.1 0.1 fusion.22
  126.3 0.6 collective-permute-done.11
  126.9 1.1 multiply_reduce_fusion
  129.2 42.2 %all-reduce.6 = (f32[]{:T(128)}, f32[]{:T(128)}, f32[]{:T(128)}, f32[]{:T(128)}, f32[]{:T(128)}, /*index=5*/f32[]{:T(128)}, f32[]{:T(128)}, f32[]{:T(128)}) all-reduce(f32[]{:T(128)} %get-tuple-element.8, f32[]{:T(128)} %get-tuple-element.10, f32[]{:T(128)} %get-tuple-element.7, ...), channel_id=1, replica_groups=mesh['layer'=8,'split'=4] {'layer','split'}, use_global_device_ids=true, to_apply=%region_5.6 | all-reduce | flops 8 | bytes 64 | tf_op jit(solution)/shard_map/psum | solution.py:292
  176.6 0.9 multiply_subtract_fusion
  (15 shorter events, 0.1 us)
Async XLA Ops:
  1.5 109.6 %collective-permute-start.4 = (f32[1,128,128]{2,1,0:T(8,128)S(1)}, f32[1,128,128]{2,1,0:T(8,128)S(1)}, u32[]{:S(2)}, u32[]{:S(2)}) collective-permute-start(f32[1,128,128]{2,1,0:T(8,128)S(1)} %get-tuple-element.33), channel_id=1, source_target_pairs={{4,0},{8,4},{12,8},{16,12},{20,16},{24,20},{28,24},{5,1},{9,5},{13... | collective-permute-start | bytes 196616 | tf_op jit(solution)/shard_map/ppermute | solution.py:272
  2.8 108.2 %collective-permute-start.5 = (f32[1,128,128]{2,1,0:T(8,128)S(1)}, f32[1,128,128]{2,1,0:T(8,128)S(1)}, u32[]{:S(2)}, u32[]{:S(2)}) collective-permute-start(f32[1,128,128]{2,1,0:T(8,128)S(1)} %get-tuple-element.34), channel_id=1, source_target_pairs={{0,4},{4,8},{8,12},{12,16},{16,20},{20,24},{24,28},{1,5},{5,9},{9,... | collective-permute-start | bytes 196616 | tf_op jit(solution)/shard_map/ppermute | solution.py:271
  98.1 3.5 %copy-start.1 = (f32[4,128,128]{2,1,0:T(8,128)S(1)}, f32[4,128,128]{2,1,0:T(8,128)}, u32[]{:S(2)}) copy-start(f32[4,128,128]{2,1,0:T(8,128)} %shard_map.50) | copy-start | bytes 786436
  99.0 5.0 %collective-permute-start.1 = (f32[1,128,128]{2,1,0:T(8,128)S(1)}, f32[1,128,128]{2,1,0:T(8,128)S(1)}, u32[]{:S(2)}, u32[]{:S(2)}) collective-permute-start(f32[1,128,128]{2,1,0:T(8,128)S(1)} %get-tuple-element.39), channel_id=1, source_target_pairs={{0,4},{4,8},{8,12},{12,16},{16,20},{20,24},{24,28},{1,5},{5,9},{9,... | collective-permute-start | bytes 196616 | tf_op jit(solution)/shard_map/ppermute | solution.py:271
  100.3 6.4 %collective-permute-start = (f32[1,128,128]{2,1,0:T(8,128)S(1)}, f32[1,128,128]{2,1,0:T(8,128)S(1)}, u32[]{:S(2)}, u32[]{:S(2)}) collective-permute-start(f32[1,128,128]{2,1,0:T(8,128)S(1)} %get-tuple-element.40), channel_id=1, source_target_pairs={{4,0},{8,4},{12,8},{16,12},{20,16},{24,20},{28,24},{5,1},{9,5},{13... | collective-permute-start | bytes 196616 | tf_op jit(solution)/shard_map/ppermute | solution.py:272
  101.6 1.0 copy-start
  106.7 4.4 %collective-permute-start.2 = (f32[6,1,128]{2,1,0:T(1,128)S(1)}, f32[6,1,128]{2,1,0:T(1,128)S(1)}, u32[]{:S(2)}, u32[]{:S(2)}) collective-permute-start(f32[6,1,128]{2,1,0:T(1,128)S(1)} %get-tuple-element.27), channel_id=1, source_target_pairs={{1,0},{2,1},{3,2},{5,4},{6,5},{7,6},{9,8},{10,9},{11,10},{13,12},{... | collective-permute-start | bytes 9224 | tf_op jit(solution)/shard_map/ppermute | solution.py:272
  108.0 3.8 %collective-permute-start.3 = (f32[6,1,128]{2,1,0:T(1,128)S(1)}, f32[6,1,128]{2,1,0:T(1,128)S(1)}, u32[]{:S(2)}, u32[]{:S(2)}) collective-permute-start(f32[6,1,128]{2,1,0:T(1,128)S(1)} %get-tuple-element.28), channel_id=1, source_target_pairs={{0,1},{1,2},{2,3},{4,5},{5,6},{6,7},{8,9},{9,10},{10,11},{12,13},{... | collective-permute-start | bytes 9224 | tf_op jit(solution)/shard_map/ppermute | solution.py:271
  111.1 1.0 copy-start.2
  112.2 7.8 %collective-permute-start.9 = (f32[1,128,128]{2,1,0:T(8,128)S(1)}, f32[1,128,128]{2,1,0:T(8,128)S(1)}, u32[]{:S(2)}, u32[]{:S(2)}) collective-permute-start(f32[1,128,128]{2,1,0:T(8,128)S(1)} %get-tuple-element.29), channel_id=1, source_target_pairs={{0,4},{4,8},{8,12},{12,16},{16,20},{20,24},{24,28},{1,5},{5,9},{9,... | collective-permute-start | bytes 196616 | tf_op jit(solution)/shard_map/ppermute | solution.py:271
  113.9 6.8 %collective-permute-start.8 = (f32[1,128,128]{2,1,0:T(8,128)S(1)}, f32[1,128,128]{2,1,0:T(8,128)S(1)}, u32[]{:S(2)}, u32[]{:S(2)}) collective-permute-start(f32[1,128,128]{2,1,0:T(8,128)S(1)} %get-tuple-element.30), channel_id=1, source_target_pairs={{4,0},{8,4},{12,8},{16,12},{20,16},{24,20},{28,24},{5,1},{9,5},{13... | collective-permute-start | bytes 196616 | tf_op jit(solution)/shard_map/ppermute | solution.py:272
  115.2 11.1 %collective-permute-start.6 = (f32[6,1,128]{2,1,0:T(1,128)S(1)}, f32[6,1,128]{2,1,0:T(1,128)S(1)}, u32[]{:S(2)}, u32[]{:S(2)}) collective-permute-start(f32[6,1,128]{2,1,0:T(1,128)S(1)} %get-tuple-element.25), channel_id=1, source_target_pairs={{1,0},{2,1},{3,2},{5,4},{6,5},{7,6},{9,8},{10,9},{11,10},{13,12},{... | collective-permute-start | bytes 9224 | tf_op jit(solution)/shard_map/ppermute | solution.py:272
  116.5 9.8 %collective-permute-start.7 = (f32[6,1,128]{2,1,0:T(1,128)S(1)}, f32[6,1,128]{2,1,0:T(1,128)S(1)}, u32[]{:S(2)}, u32[]{:S(2)}) collective-permute-start(f32[6,1,128]{2,1,0:T(1,128)S(1)} %get-tuple-element.26), channel_id=1, source_target_pairs={{0,1},{1,2},{2,3},{4,5},{5,6},{6,7},{8,9},{9,10},{10,11},{12,13},{... | collective-permute-start | bytes 9224 | tf_op jit(solution)/shard_map/ppermute | solution.py:271
  120.7 5.6 %collective-permute-start.10 = (f32[6,1,128]{2,1,0:T(1,128)S(1)}, f32[6,1,128]{2,1,0:T(1,128)S(1)}, u32[]{:S(2)}, u32[]{:S(2)}) collective-permute-start(f32[6,1,128]{2,1,0:T(1,128)S(1)} %get-tuple-element.23), channel_id=1, source_target_pairs={{1,0},{2,1},{3,2},{5,4},{6,5},{7,6},{9,8},{10,9},{11,10},{13,12},{... | collective-permute-start | bytes 9224 | tf_op jit(solution)/shard_map/ppermute | solution.py:272
  122.0 5.0 %collective-permute-start.11 = (f32[6,1,128]{2,1,0:T(1,128)S(1)}, f32[6,1,128]{2,1,0:T(1,128)S(1)}, u32[]{:S(2)}, u32[]{:S(2)}) collective-permute-start(f32[6,1,128]{2,1,0:T(1,128)S(1)} %get-tuple-element.24), channel_id=1, source_target_pairs={{0,1},{1,2},{2,3},{4,5},{5,6},{6,7},{8,9},{9,10},{10,11},{12,13},{... | collective-permute-start | bytes 9224 | tf_op jit(solution)/shard_map/ppermute | solution.py:271

commit v2 on v1

--- a/solution.py
+++ b/solution.py
@@ -26,8 +26,10 @@
 
 
 def sweep_kernel(
-    depth, parts, rs_ref, inv_ref, out_ref,
+    depth, parts, rs_ref, diag_ref, inv_ref, sol_ref, res_ref,
     mf, mhi, mlo, whi, wlo, uhi, ulo, loc, base, rsend, rrecv, vin, vout, din, dout, dsend, drecv,
+    arhs, dirn, img, aimg, zh, xh, xs, srow, sall, trow, tall,
+    hs_sem, hr_sem, ls_sem, lr_sem, ts_sem, tr_sem,
     own_sem, gs_sem, gr_sem, as_sem, ar_sem, bs_sem, br_sem, vs_sem, vr_sem, ds_sem, dr_sem,
 ):
     planes, nx, xb = inv_ref.shape
@@ -38,11 +40,102 @@
     l, s = lax.axis_index("layer"), lax.axis_index("split")
     bits = [1 << i for i in range(parts.bit_length() - 1)]
 
+    last = planes - 1
+    row_at = lax.broadcasted_iota(jnp.int32, (xb, ny), 0)
+    col_at = lax.broadcasted_iota(jnp.int32, (xb, ny), 1)
+
+    def stage_lines(h, ref):
+        for k in range(planes):
+            xs[h, 0, k:k + 1] = ref[k, 0:1]
+            xs[h, 1, k:k + 1] = ref[k, xb - 1:xb]
+
+    def halo_copies(h, ref):
+        def zcopy(side, slot):
+            return pltpu.make_async_remote_copy(
+                src_ref=ref.at[0 if side == 0 else last], dst_ref=zh.at[h, slot], send_sem=hs_sem.at[h, side],
+                recv_sem=hr_sem.at[h, slot],
+                device_id=(lax.rem(l + 2 * side - 1 + depth, depth), s), device_id_type=MESH)
+
+        def xcopy(side, slot):
+            return pltpu.make_async_remote_copy(
+                src_ref=xs.at[h, side], dst_ref=xh.at[h, slot], send_sem=hs_sem.at[h, 2 + side],
+                recv_sem=hr_sem.at[h, 2 + slot],
+                device_id=(l, lax.rem(s + 2 * side - 1 + parts, parts)), device_id_type=MESH)
+
+        out = []
+        for side in range(2):
+            zhas = l > 0 if side == 0 else l < depth - 1
+            xhas = s > 0 if side == 0 else s < parts - 1
+            for has, copy, slot in ((zhas, zcopy, zh), (xhas, xcopy, xh)):
+                out.append((
+                    has, functools.partial(copy, side, 1 - side), functools.partial(copy, side, side),
+                    slot.at[h, side]))
+        return out
+
+    def halo_start(h, ref):
+        for has, copy, _, _ in halo_copies(h, ref):
+            @pl.when(has)
+            def _():
+                copy().start()
+
+    def halo_wait(h, ref):
+        for has, _, back, slot in halo_copies(h, ref):
+            @pl.when(has)
+            def _():
+                back().wait_recv()
+
+            @pl.when(jnp.logical_not(has))
+            def _():
+                slot[...] = jnp.zeros_like(slot[...])
+
+    def halo_finish(h, ref):
+        for has, copy, _, _ in halo_copies(h, ref):
+            @pl.when(has)
+            def _():
+                copy().wait_send()
+
+    def apply_operator(h, ref, dst):
+        for k in range(planes):
+            v = ref[k]
+            before = zh[h, 0] if k == 0 else ref[k - 1]
+            after = zh[h, 1] if k == last else ref[k + 1]
+            beside = before + after
+            beside += jnp.where(row_at == 0, xh[h, 0, k:k + 1], pltpu.roll(v, 1, 0))
+            beside += jnp.where(row_at == xb - 1, xh[h, 1, k:k + 1], pltpu.roll(v, xb - 1, 0))
+            beside += jnp.where(col_at == 0, 0.0, pltpu.roll(v, 1, 1))
+            beside += jnp.where(col_at == ny - 1, 0.0, pltpu.roll(v, ny - 1, 1))
+            dst[k] = (6.0 + diag_ref[k]) * v - beside
+
+    lane = lax.broadcasted_iota(jnp.int32, (1, ny), 1)
+
+    def summed(pairs):
+        row = jnp.zeros((1, ny), F32)
+        for i, (a, b) in enumerate(pairs):
+            acc = a[0] * b[0]
+            for k in range(1, planes):
+                acc = acc + a[k] * b[k]
+            total = jnp.sum(jnp.sum(acc, axis=0, keepdims=True), axis=1, keepdims=True)
+            row = jnp.where(lane == i, total, row)
+        return row
+
+    def spread_layer(r, back):
+        to = lax.rem(l + r, depth)
+        slot = lax.rem(l + depth - r, depth) if back else l
+        return pltpu.make_async_remote_copy(
+            src_ref=srow, dst_ref=sall.at[slot], send_sem=ls_sem.at[r], recv_sem=lr_sem.at[r],
+            device_id=(to, s), device_id_type=MESH)
+
+    def spread_split(r, back):
+        slot = s ^ r if back else s
+        return pltpu.make_async_remote_copy(
+            src_ref=trow, dst_ref=tall.at[slot], send_sem=ts_sem.at[r], recv_sem=tr_sem.at[r],
+            device_id=(l, s ^ r), device_id_type=MESH)
+
     barrier = pltpu.get_barrier_semaphore()
     for r in range(1, parts):
         pl.semaphore_signal(barrier, inc=1, device_id=(l, s ^ r), device_id_type=MESH)
-    pl.semaphore_signal(barrier, inc=1, device_id=(lax.rem(l + 1, depth), s), device_id_type=MESH)
-    pl.semaphore_signal(barrier, inc=1, device_id=(lax.rem(l + depth - 1, depth), s), device_id_type=MESH)
+    for r in range(1, depth):
+        pl.semaphore_signal(barrier, inc=1, device_id=(lax.rem(l + r, depth), s), device_id_type=MESH)
 
     def own_copy(k):
         return pltpu.make_async_copy(inv_ref.at[k], mf.at[k, s], own_sem.at[k])
@@ -53,7 +146,8 @@
         turned = jnp.transpose(rs_ref[k])
         for r in range(parts):
             rsend[r, k] = turned[r * yb:(r + 1) * yb]
-    pl.semaphore_wait(barrier, parts + 1)
+    stage_lines(0, rs_ref)
+    pl.semaphore_wait(barrier, parts + depth - 2)
 
     def regroup(src, dst, ssem, rsem, r):
         return pltpu.make_async_remote_copy(
@@ -81,6 +175,7 @@
     for k in range(planes):
         for b in reversed(bits):
             shift(k, 0, b).start()
+    halo_start(0, rs_ref)
     rrecv[s] = rsend[s]
     for r in range(1, parts):
         regroup_in(rsend, rrecv, as_sem, ar_sem, r).wait_recv()
@@ -102,6 +197,8 @@
 
     half = nx // 2
 
+    halo_wait(0, rs_ref)
+    apply_operator(0, rs_ref, arhs)
     fetch(0)
     for j in range(parts):
         hi, lo = halves(jnp.transpose(mf[0, j]))
@@ -118,8 +215,6 @@
             hi, lo = halves(product(whi[k - 1, rows], wlo[k - 1, rows], mhi[k], mlo[k], 1))
             whi[k, rows] = hi
             wlo[k, rows] = lo
-
-    last = planes - 1
 
     def hop(src, dst, ssem, rsem, c, step):
         return pltpu.make_async_remote_copy(
@@ -214,7 +309,55 @@
     for r in range(1, parts):
         regroup_in(dsend, drecv, bs_sem, br_sem, r).wait_recv()
     for k in range(planes):
-        out_ref[k] = jnp.transpose(jnp.concatenate([drecv[j, k] for j in range(parts)], axis=0))
+        dirn[k] = jnp.transpose(jnp.concatenate([drecv[j, k] for j in range(parts)], axis=0))
+
+    stage_lines(1, dirn)
+    halo_start(1, dirn)
+    halo_wait(1, dirn)
+    apply_operator(1, dirn, img)
+    stage_lines(2, img)
+    halo_start(2, img)
+    halo_wait(2, img)
+    apply_operator(2, img, aimg)
+    srow[...] = summed([
+        (rs_ref, rs_ref), (rs_ref, img), (arhs, rs_ref), (arhs, img), (aimg, rs_ref), (aimg, img),
+        (arhs, arhs), (arhs, aimg), (aimg, aimg)])
+    for r in range(1, depth):
+        spread_layer(r, False).start()
+    sall[l] = srow[...]
+    for r in range(1, depth):
+        spread_layer(r, True).wait_recv()
+    row = sall[0]
+    for i in range(1, depth):
+        row = row + sall[i]
+    trow[...] = row
+    for r in range(1, parts):
+        spread_split(r, False).start()
+    tall[s] = trow[...]
+    for r in range(1, parts):
+        spread_split(r, True).wait_recv()
+    row = tall[0]
+    for i in range(1, parts):
+        row = row + tall[i]
+
+    def total(i):
+        return jnp.sum(jnp.where(lane == i, row, 0.0), axis=1, keepdims=True)
+
+    alpha = total(0) / total(1)
+    cross = total(2) - alpha * (total(3) + total(4)) + alpha * alpha * total(5)
+    own = total(6) - 2.0 * alpha * total(7) + alpha * alpha * total(8)
+    omega = cross / own
+    for k in range(planes):
+        middle = rs_ref[k] - alpha * img[k]
+        sol_ref[k] = alpha * dirn[k] + omega * middle
+        res_ref[k] = middle - omega * (arhs[k] - alpha * aimg[k])
+
+    for h, ref in ((0, rs_ref), (1, dirn), (2, img)):
+        halo_finish(h, ref)
+    for r in range(1, depth):
+        spread_layer(r, False).wait_send()
+    for r in range(1, parts):
+        spread_split(r, False).wait_send()
 
     for r in range(1, parts):
         regroup(rsend, rrecv, as_sem, ar_sem, r).wait_send()
@@ -232,7 +375,7 @@
             hop(dout, din, ds_sem, dr_sem, c, -1).wait_send()
 
 
-def sweep(right_side, inverses):
+def per_device(right_side, diagonal, inverses):
     depth, parts = lax.axis_size("layer"), lax.axis_size("split")
     planes, nx, xb = inverses.shape
     ny = right_side.shape[2]
@@ -243,88 +386,29 @@
     pieces = pltpu.VMEM((parts, planes, yb, xb), F32)
     carry = pltpu.VMEM((chunks, yb // chunks, nx), F32)
     dma = pltpu.SemaphoreType.DMA
+    field = pltpu.VMEM(right_side.shape, F32)
+    plane = right_side.shape[1:]
     return pl.pallas_call(
         functools.partial(sweep_kernel, depth, parts),
-        out_shape=jax.ShapeDtypeStruct(right_side.shape, F32),
-        in_specs=[pl.BlockSpec(memory_space=pltpu.VMEM)] * 2,
-        out_specs=pl.BlockSpec(memory_space=pltpu.VMEM),
+        out_shape=[jax.ShapeDtypeStruct(right_side.shape, F32)] * 2,
+        in_specs=[pl.BlockSpec(memory_space=pltpu.VMEM)] * 3,
+        out_specs=[pl.BlockSpec(memory_space=pltpu.VMEM)] * 2,
         scratch_shapes=[
             pltpu.VMEM((planes, parts, nx, xb), F32),
             square, square, square, square, square, square,
             lines, lines, pieces, pieces, carry, carry, carry, carry, pieces, pieces,
+            field, field, field, field,
+            pltpu.VMEM((3, 2) + plane, F32), pltpu.VMEM((3, 2, planes, ny), F32), pltpu.VMEM((3, 2, planes, ny), F32),
+            pltpu.VMEM((1, ny), F32), pltpu.VMEM((depth, 1, ny), F32),
+            pltpu.VMEM((1, ny), F32), pltpu.VMEM((parts, 1, ny), F32),
+            dma((3, 4)), dma((3, 4)), dma((depth,)), dma((depth,)), dma((parts,)), dma((parts,)),
             dma((planes,)), dma((planes, parts)), dma((planes, parts)),
             dma((parts,)), dma((parts,)), dma((parts,)), dma((parts,)),
             dma((chunks,)), dma((chunks,)), dma((chunks,)), dma((chunks,)),
         ],
         compiler_params=pltpu.CompilerParams(
             collective_id=0, has_side_effects=True, vmem_limit_bytes=60 * 1024 * 1024),
-    )(right_side, inverses)
-
-
-def with_halo(x, sides, width):
-    for axis, dim in sides:
-        size, length = (lax.axis_size(axis), x.shape[dim])
-        up = [(i, (i + 1) % size) for i in range(size - 1)]
-        down = [(j, i) for i, j in up]
-        last = lax.slice_in_dim(x, length - width, length, axis=dim)
-        first = lax.slice_in_dim(x, 0, width, axis=dim)
-        before = lax.ppermute(last, axis, up)
-        after = lax.ppermute(first, axis, down)
-        x = jnp.concatenate([before, x, after], axis=dim)
-    return x
-
-
-def stencil(values, diagonal):
-    padded = with_halo(values, (("layer", 0), ("split", 1)), 1)
-    beside = padded[2:, 1:-1, :] + padded[:-2, 1:-1, :]
-    beside = beside + padded[1:-1, 2:, :] + padded[1:-1, :-2, :]
-    centre_part = padded[1:-1, 1:-1, :]
-    y_upper = jnp.pad(centre_part[:, :, 1:], ((0, 0), (0, 0), (0, 1)))
-    y_lower = jnp.pad(centre_part[:, :, :-1], ((0, 0), (0, 0), (1, 0)))
-    return (6.0 + diagonal) * values - beside - y_upper - y_lower
-
-
-def per_device(right_side, diagonal, inverses):
-    applied_rhs = stencil(right_side, diagonal)
-    direction = sweep(right_side, inverses)
-    image = stencil(direction, diagonal)
-    applied_image = stencil(image, diagonal)
-    sums_all = lax.psum(
-        (
-            jnp.sum(right_side * right_side),
-            jnp.sum(right_side * image),
-            jnp.sum(applied_rhs * right_side),
-            jnp.sum(applied_rhs * image),
-            jnp.sum(applied_image * right_side),
-            jnp.sum(applied_image * image),
-            jnp.sum(applied_rhs * applied_rhs),
-            jnp.sum(applied_rhs * applied_image),
-            jnp.sum(applied_image * applied_image),
-        ),
-        ("layer", "split"),
-    )
-    (
-        norm_sq,
-        curv_sum,
-        rhs_rhs,
-        rhs_image,
-        image_rhs,
-        image_image,
-        arhs_arhs,
-        arhs_aimage,
-        aimage_aimage,
-    ) = sums_all
-    step_alpha = norm_sq / curv_sum
-    middle = right_side - step_alpha * image
-    tangent = applied_rhs - step_alpha * applied_image
-    cross_sum = (
-        rhs_rhs - step_alpha * (rhs_image + image_rhs) + step_alpha * step_alpha * image_image
-    )
-    self_sum = arhs_arhs - 2.0 * step_alpha * arhs_aimage + step_alpha * step_alpha * aimage_aimage
-    step_omega = cross_sum / self_sum
-    solution_field = step_alpha * direction + step_omega * middle
-    residual = middle - step_omega * tangent
-    return (solution_field, residual)
+    )(right_side, diagonal, inverses)
 
 
 def solution(mesh):

time: 178 us -> 119 us (0.67)
  blocking collectives: 42.2 us -> 0 us
  starting transfers between devices: 26.8 us -> 0 us
  Pallas kernels: 89.7 us -> 115 us
  between operations: 7.19 us -> 0.65 us
  waiting for transfers between devices: 6.1 us -> 0 us
  other arithmetic: 2.13 us -> 0 us
    psum x1 -> x0, blocking collectives: 42.2 us -> none  [per_device(): lax.psum((jnp.sum(right_side * right_side), jnp.sum(right_side * image),...]
    ppermute x12 -> x0, starting transfers between devices: 26.8 us -> none  [the longest x6 19.1 us: with_halo(): before = lax.ppermute(last, axis, up)]
    pallas_call x1, Pallas kernels: 89.7 us -> 115 us  [per_device(): pl.pallas_call(functools.partial(sweep_kernel, depth, parts), out_shape=[...]
    ppermute x12 -> x0, waiting for transfers between devices: 6.1 us -> none  [the longest x6 3.41 us: with_halo(): after = lax.ppermute(first, axis, down)]
    slice x7 -> x0, local copies, waits for them, and re-layouts: 2.21 us -> none  [the longest x2 0.94 us: with_halo(): last = lax.slice_in_dim(x, length - width, length, axis=dim)]
  transfers between devices with their start and end apart: 12 -> 0, of which waited for: 5 -> 0; matrix products, arithmetic and copies ran while one was open for 1% -> 0% of each run, Pallas kernels for 51% -> 0%
where the time goes in v2:
time: 119 us; the launch traced here: 118 us
  Pallas kernels  115 us (97%)
  local copies, waits for them, and re-layouts  2.42 us (2%)
    pallas_call x1, Pallas kernels, per_device(): pl.pallas_call(functools.partial(sweep_kernel, depth, parts), out_shape=[...  115 us
    unnamed x4, local copies, waits for them, and re-layouts  2.42 us

profile of v2, /device:TPU:0, one launch (start us, length us, event | category | flops | bytes accessed | tf_op | source)
XLA Modules:
  0.0 118.4 jit_solution(17633870993890554659)
XLA Ops:
  0.6 115.3 %shard_map.50 = (f32[4,128,128]{2,1,0:T(8,128)}, f32[4,128,128]{2,1,0:T(8,128)}) custom-call(f32[4,128,128]{2,1,0:T(8,128)} %rs_ref.1, f32[4,128,128]{2,1,0:T(8,128)} %diag_ref.1, f32[4,512,128]{2,1,0:T(8,128)} %inv_ref.1), custom_call_target="tpu_custom_call" | custom-call | tf_op jit(solution)/shard_map/pallas_call | solution.py:391
  115.9 0.0 copy-start
  115.9 1.7 %copy.7 = f32[4,128,128]{2,1,0:T(8,128)} copy(f32[4,128,128]{2,1,0:T(8,128)} %get-tuple-element.4) | data formatting | bytes 524288
  117.7 0.0 copy-done
  117.7 0.7 copy.8
Async XLA Ops:
  115.9 1.7 %copy-start = (f32[4,128,128]{2,1,0:T(8,128)S(1)}, f32[4,128,128]{2,1,0:T(8,128)}, u32[]{:S(2)}) copy-start(f32[4,128,128]{2,1,0:T(8,128)} %get-tuple-element.5) | copy-start | bytes 786436

commit v3 on v2

--- a/solution.py
+++ b/solution.py
@@ -159,33 +159,46 @@
             src_ref=src.at[s ^ r], dst_ref=dst.at[s ^ r], send_sem=ssem.at[r], recv_sem=rsem.at[r],
             device_id=(l, s ^ r), device_id_type=MESH)
 
-    def shift(k, r, b):
-        src = inv_ref.at[k] if r == 0 else mf.at[k, s ^ r]
-        return pltpu.make_async_remote_copy(
-            src_ref=src, dst_ref=mf.at[k, s ^ r], send_sem=gs_sem.at[k, r ^ b], recv_sem=gr_sem.at[k, r ^ b],
+    cuts = 2
+    cut = nx // cuts
+
+    def shift(k, h, r, b):
+        rows = pl.ds(h * cut, cut)
+        src = inv_ref.at[k, rows] if r == 0 else mf.at[k, s ^ r, rows]
+        return pltpu.make_async_remote_copy(
+            src_ref=src, dst_ref=mf.at[k, s ^ r, rows],
+            send_sem=gs_sem.at[k * cuts + h, r ^ b], recv_sem=gr_sem.at[k * cuts + h, r ^ b],
             device_id=(l, s ^ b), device_id_type=MESH)
 
-    def arrived(k, r):
-        return pltpu.make_async_remote_copy(
-            src_ref=mf.at[k, s ^ r], dst_ref=mf.at[k, s ^ r], send_sem=gs_sem.at[k, r], recv_sem=gr_sem.at[k, r],
+    def arrived(k, h, r):
+        rows = pl.ds(h * cut, cut)
+        return pltpu.make_async_remote_copy(
+            src_ref=mf.at[k, s ^ r, rows], dst_ref=mf.at[k, s ^ r, rows],
+            send_sem=gs_sem.at[k * cuts + h, r], recv_sem=gr_sem.at[k * cuts + h, r],
             device_id=(l, s ^ 1), device_id_type=MESH)
 
     for r in range(1, parts):
         regroup(rsend, rrecv, as_sem, ar_sem, r).start()
-    for k in range(planes):
+    halo_start(0, rs_ref)
+    for h in range(cuts):
         for b in reversed(bits):
-            shift(k, 0, b).start()
-    halo_start(0, rs_ref)
+            shift(0, h, 0, b).start()
     rrecv[s] = rsend[s]
     for r in range(1, parts):
         regroup_in(rsend, rrecv, as_sem, ar_sem, r).wait_recv()
 
     def fetch(k):
-        for r in range(1, parts):
-            arrived(k, r).wait_recv()
-            for b in bits:
-                if b < (r & -r):
-                    shift(k, r, b).start()
+        for h in range(cuts):
+            for r in range(1, parts):
+                arrived(k, h, r).wait_recv()
+                for b in bits:
+                    if b < (r & -r):
+                        shift(k, h, r, b).start()
+                if r == bits[-1]:
+                    @pl.when(k < last)
+                    def _():
+                        for b in reversed(bits):
+                            shift(k + 1, h, 0, b).start()
         own_copy(k).wait()
         for j in range(parts):
             hi, lo = halves(mf[k, j])
@@ -197,8 +210,11 @@
 
     half = nx // 2
 
-    halo_wait(0, rs_ref)
-    apply_operator(0, rs_ref, arhs)
+    def hop(src, dst, ssem, rsem, c, step):
+        return pltpu.make_async_remote_copy(
+            src_ref=src.at[c], dst_ref=dst.at[c], send_sem=ssem.at[c], recv_sem=rsem.at[c],
+            device_id=(lax.rem(l + step + depth, depth), s), device_id_type=MESH)
+
     fetch(0)
     for j in range(parts):
         hi, lo = halves(jnp.transpose(mf[0, j]))
@@ -206,33 +222,32 @@
         wlo[0, j * xb:(j + 1) * xb] = lo
     loc[0] = product(*halves(source(0)), mhi[0], mlo[0], 1)
 
+    halo_wait(0, rs_ref)
+    apply_operator(0, rs_ref, arhs)
+
     @pl.loop(1, planes)
     def _(k):
         fetch(k)
         loc[k] = product(*halves(source(k) + loc[k - 1]), mhi[k], mlo[k], 1)
+
+        @pl.when(jnp.logical_and(k == last, l == 0))
+        def _():
+            for c in range(chunks):
+                vin[c] = jnp.zeros_like(vin[c])
+                vout[c] = loc[last, c * cb:(c + 1) * cb]
+            for c in range(chunks):
+                hop(vout, vin, vs_sem, vr_sem, c, 1).start()
+
         for t in range(2):
             rows = slice(t * half, (t + 1) * half)
             hi, lo = halves(product(whi[k - 1, rows], wlo[k - 1, rows], mhi[k], mlo[k], 1))
             whi[k, rows] = hi
             wlo[k, rows] = lo
 
-    def hop(src, dst, ssem, rsem, c, step):
-        return pltpu.make_async_remote_copy(
-            src_ref=src.at[c], dst_ref=dst.at[c], send_sem=ssem.at[c], recv_sem=rsem.at[c],
-            device_id=(lax.rem(l + step + depth, depth), s), device_id_type=MESH)
-
     def down_chain():
         for c in range(chunks):
             rows = slice(c * cb, (c + 1) * cb)
-
-            @pl.when(l > 0)
-            def _():
-                hop(vout, vin, vs_sem, vr_sem, c, 1).wait_recv()
-
-            @pl.when(l == 0)
-            def _():
-                vin[c] = jnp.zeros_like(vin[c])
-
+            hop(vout, vin, vs_sem, vr_sem, c, 1).wait_recv()
             vout[c] = loc[last, rows] + product(*halves(vin[c]), whi[last], wlo[last], 0)
 
             @pl.when(l < depth - 1)
@@ -263,7 +278,7 @@
 
     @pl.loop(0, 2)
     def _(turn):
-        @pl.when(turn != early)
+        @pl.when(jnp.logical_and(turn != early, l > 0))
         def _():
             down_chain()
 
@@ -364,7 +379,8 @@
         regroup(dsend, drecv, bs_sem, br_sem, r).wait_send()
     for k in range(planes):
         for r in range(1, parts):
-            arrived(k, r).wait_send()
+            for h in range(cuts):
+                arrived(k, h, r).wait_send()
     for c in range(chunks):
         @pl.when(l < depth - 1)
         def _():
@@ -380,7 +396,7 @@
     planes, nx, xb = inverses.shape
     ny = right_side.shape[2]
     yb = ny // parts
-    chunks = 2 if yb % 16 == 0 else 1
+    chunks = yb // 8 if yb % 8 == 0 else 1
     square = pltpu.VMEM((planes, nx, nx), BF16)
     lines = pltpu.VMEM((planes, yb, nx), F32)
     pieces = pltpu.VMEM((parts, planes, yb, xb), F32)
@@ -402,7 +418,7 @@
             pltpu.VMEM((1, ny), F32), pltpu.VMEM((depth, 1, ny), F32),
             pltpu.VMEM((1, ny), F32), pltpu.VMEM((parts, 1, ny), F32),
             dma((3, 4)), dma((3, 4)), dma((depth,)), dma((depth,)), dma((parts,)), dma((parts,)),
-            dma((planes,)), dma((planes, parts)), dma((planes, parts)),
+            dma((planes,)), dma((planes * 2, parts)), dma((planes * 2, parts)),
             dma((parts,)), dma((parts,)), dma((parts,)), dma((parts,)),
             dma((chunks,)), dma((chunks,)), dma((chunks,)), dma((chunks,)),
         ],

time: 119 us -> 109 us (0.916)
  Pallas kernels: 115 us -> 106 us
    pallas_call x1, Pallas kernels: 115 us -> 106 us  [per_device(): pl.pallas_call(functools.partial(sweep_kernel, depth, parts), out_shape=[...]
where the time goes in v3:
time: 109 us
  Pallas kernels  106 us (97%)
  local copies, waits for them, and re-layouts  2.42 us (2%)
    pallas_call x1, Pallas kernels, per_device(): pl.pallas_call(functools.partial(sweep_kernel, depth, parts), out_shape=[...  106 us
    unnamed x4, local copies, waits for them, and re-layouts  2.42 us

profile of v3, /device:TPU:0, one launch (start us, length us, event | category | flops | bytes accessed | tf_op | source)
XLA Modules:
  0.0 108.8 jit_solution(1310849752957194676)
XLA Ops:
  0.6 105.7 %shard_map.50 = (f32[4,128,128]{2,1,0:T(8,128)}, f32[4,128,128]{2,1,0:T(8,128)}) custom-call(f32[4,128,128]{2,1,0:T(8,128)} %rs_ref.1, f32[4,128,128]{2,1,0:T(8,128)} %diag_ref.1, f32[4,512,128]{2,1,0:T(8,128)} %inv_ref.1), custom_call_target="tpu_custom_call" | custom-call | tf_op jit(solution)/shard_map/pallas_call | solution.py:407
  106.3 0.0 copy-start
  106.4 1.7 %copy.7 = f32[4,128,128]{2,1,0:T(8,128)} copy(f32[4,128,128]{2,1,0:T(8,128)} %get-tuple-element.4) | data formatting | bytes 524288
  108.1 0.0 copy-done
  108.1 0.7 copy.8
Async XLA Ops:
  106.3 1.7 %copy-start = (f32[4,128,128]{2,1,0:T(8,128)S(1)}, f32[4,128,128]{2,1,0:T(8,128)}, u32[]{:S(2)}) copy-start(f32[4,128,128]{2,1,0:T(8,128)} %get-tuple-element.5) | copy-start | bytes 786436

commit v4 on v3

--- a/solution.py
+++ b/solution.py
@@ -28,6 +28,7 @@
 def sweep_kernel(
     depth, parts, rs_ref, diag_ref, inv_ref, sol_ref, res_ref,
     mf, mhi, mlo, whi, wlo, uhi, ulo, loc, base, rsend, rrecv, vin, vout, din, dout, dsend, drecv,
+    usend, uland, phi, plo, vhi, vlo, bodd, cst, pin, us_sem, ur_sem, bo_s, bo_r, ps_sem, pr_sem,
     arhs, dirn, img, aimg, zh, xh, xs, srow, sall, trow, tall,
     hs_sem, hr_sem, ls_sem, lr_sem, ts_sem, tr_sem,
     own_sem, gs_sem, gr_sem, as_sem, ar_sem, bs_sem, br_sem, vs_sem, vr_sem, ds_sem, dr_sem,
@@ -254,6 +255,26 @@
             def _():
                 hop(vout, vin, vs_sem, vr_sem, c, 1).start()
 
+    odd = l % 2 == 1
+    even = jnp.logical_not(odd)
+    mine = pl.ds((s % 2) * half, half)
+    other = pl.ds((1 - s % 2) * half, half)
+
+    def pair_map():
+        return pltpu.make_async_remote_copy(
+            src_ref=usend.at[mine], dst_ref=uland.at[mine], send_sem=us_sem.at[0], recv_sem=ur_sem.at[0],
+            device_id=(l ^ 1, s), device_id_type=MESH)
+
+    def mate_map(rows):
+        return pltpu.make_async_remote_copy(
+            src_ref=uland.at[rows], dst_ref=uland.at[rows], send_sem=us_sem.at[1], recv_sem=ur_sem.at[1],
+            device_id=(l, s ^ 1), device_id_type=MESH)
+
+    def pair_base():
+        return pltpu.make_async_remote_copy(
+            src_ref=base.at[0], dst_ref=bodd, send_sem=bo_s.at[0], recv_sem=bo_r.at[0],
+            device_id=(l ^ 1, s), device_id_type=MESH)
+
     def compose():
         for j in range(parts):
             hi, lo = halves(jnp.transpose(mf[last, j]))
@@ -274,6 +295,11 @@
                 whi[k, rows] = hi
                 wlo[k, rows] = lo
 
+        @pl.when(odd)
+        def _():
+            usend[...] = uhi[0].astype(F32) + ulo[0].astype(F32)
+            pair_map().start()
+
     early = lax.convert_element_type(l < depth // 2, jnp.int32)
 
     @pl.loop(0, 2)
@@ -293,22 +319,61 @@
     def _(k):
         base[k] = loc[k] + product(*entering, whi[k], wlo[k], 0)
 
-    for c in range(chunks):
-        rows = slice(c * cb, (c + 1) * cb)
-
-        @pl.when(l < depth - 1)
-        def _():
-            hop(dout, din, ds_sem, dr_sem, c, -1).wait_recv()
-
-        @pl.when(l == depth - 1)
-        def _():
-            din[c] = jnp.zeros_like(din[c])
-
-        dout[c] = base[0, rows] + product(*halves(din[c]), uhi[0], ulo[0], 0)
-
-        @pl.when(l > 0)
-        def _():
-            hop(dout, din, ds_sem, dr_sem, c, -1).start()
+        @pl.when(jnp.logical_and(k == 0, odd))
+        def _():
+            pair_base().start()
+
+
+    @pl.when(odd)
+    def _():
+        for c in range(chunks):
+            @pl.when(l < depth - 1)
+            def _():
+                hop(dout, din, ds_sem, dr_sem, c, -1).wait_recv()
+
+            @pl.when(l == depth - 1)
+            def _():
+                din[c] = jnp.zeros_like(din[c])
+
+    @pl.when(even)
+    def _():
+        pair_map().wait_recv()
+        mate_map(mine).start()
+        mate_map(other).wait_recv()
+        for i in range(2):
+            rows = slice(i * half, (i + 1) * half)
+            hi, lo = halves(uland[rows])
+            phi[rows] = hi
+            plo[rows] = lo
+
+            @pl.when(l > 0)
+            def _():
+                hi, lo = halves(product(phi[rows], plo[rows], uhi[0], ulo[0], 0))
+                vhi[rows] = hi
+                vlo[rows] = lo
+
+        pair_base().wait_recv()
+        cst[...] = base[0] + product(*halves(bodd[...]), uhi[0], ulo[0], 0)
+        for c in range(chunks):
+            @pl.when(l < depth - 2)
+            def _():
+                hop(dout, pin, ps_sem, pr_sem, c, -2).wait_recv()
+
+            @pl.when(l >= depth - 2)
+            def _():
+                pin[c] = jnp.zeros_like(pin[c])
+
+            @pl.when(l > 0)
+            def _():
+                rows = slice(c * cb, (c + 1) * cb)
+                dout[c] = cst[rows] + product(*halves(pin[c]), vhi[...], vlo[...], 0)
+                hop(dout, pin, ps_sem, pr_sem, c, -2).start()
+                hop(dout, din, ds_sem, dr_sem, c, -1).start()
+
+        held = bodd[...] + product(
+            *halves(jnp.concatenate([pin[c] for c in range(chunks)], axis=0)), phi[...], plo[...], 0)
+        for c in range(chunks):
+            din[c] = held[c * cb:(c + 1) * cb]
 
     entering = halves(jnp.concatenate([din[c] for c in range(chunks)], axis=0))
 
@@ -386,9 +451,19 @@
         def _():
             hop(vout, vin, vs_sem, vr_sem, c, 1).wait_send()
 
-        @pl.when(l > 0)
-        def _():
+        @pl.when(jnp.logical_and(l > 0, even))
+        def _():
+            hop(dout, pin, ps_sem, pr_sem, c, -2).wait_send()
             hop(dout, din, ds_sem, dr_sem, c, -1).wait_send()
+
+    @pl.when(odd)
+    def _():
+        pair_map().wait_send()
+        pair_base().wait_send()
+
+    @pl.when(even)
+    def _():
+        mate_map(mine).wait_send()
 
 
 def per_device(right_side, diagonal, inverses):
@@ -397,6 +472,7 @@
     ny = right_side.shape[2]
     yb = ny // parts
     chunks = yb // 8 if yb % 8 == 0 else 1
+    flat = pltpu.VMEM((nx, nx), BF16)
     square = pltpu.VMEM((planes, nx, nx), BF16)
     lines = pltpu.VMEM((planes, yb, nx), F32)
     pieces = pltpu.VMEM((parts, planes, yb, xb), F32)
@@ -413,6 +489,9 @@
             pltpu.VMEM((planes, parts, nx, xb), F32),
             square, square, square, square, square, square,
             lines, lines, pieces, pieces, carry, carry, carry, carry, pieces, pieces,
+            pltpu.VMEM((nx, nx), F32), pltpu.VMEM((nx, nx), F32), flat, flat, flat, flat,
+            pltpu.VMEM((yb, nx), F32), pltpu.VMEM((yb, nx), F32), carry,
+            dma((2,)), dma((2,)), dma((1,)), dma((1,)), dma((chunks,)), dma((chunks,)),
             field, field, field, field,
             pltpu.VMEM((3, 2) + plane, F32), pltpu.VMEM((3, 2, planes, ny), F32), pltpu.VMEM((3, 2, planes, ny), F32),
             pltpu.VMEM((1, ny), F32), pltpu.VMEM((depth, 1, ny), F32),

time: 109 us -> 102 us (0.936)
  Pallas kernels: 106 us -> 98.4 us
    pallas_call x1, Pallas kernels: 106 us -> 98.4 us  [per_device(): pl.pallas_call(functools.partial(sweep_kernel, depth, parts), out_shape=[...]
where the time goes in v4:
time: 102 us; the launch traced here: 101 us
  Pallas kernels  98.4 us (96%)
  local copies, waits for them, and re-layouts  2.42 us (2%)
    pallas_call x1, Pallas kernels, per_device(): pl.pallas_call(functools.partial(sweep_kernel, depth, parts), out_shape=[...  98.4 us
    unnamed x4, local copies, waits for them, and re-layouts  2.42 us

profile of v4, /device:TPU:0, one launch (start us, length us, event | category | flops | bytes accessed | tf_op | source)
XLA Modules:
  0.0 101.4 jit_solution(2912482107276820876)
XLA Ops:
  0.6 98.4 %shard_map.50 = (f32[4,128,128]{2,1,0:T(8,128)}, f32[4,128,128]{2,1,0:T(8,128)}) custom-call(f32[4,128,128]{2,1,0:T(8,128)} %rs_ref.1, f32[4,128,128]{2,1,0:T(8,128)} %diag_ref.1, f32[4,512,128]{2,1,0:T(8,128)} %inv_ref.1), custom_call_target="tpu_custom_call" | custom-call | tf_op jit(solution)/shard_map/pallas_call | solution.py:483
  99.0 0.0 copy-start
  99.0 1.7 %copy.7 = f32[4,128,128]{2,1,0:T(8,128)} copy(f32[4,128,128]{2,1,0:T(8,128)} %get-tuple-element.4) | data formatting | bytes 524288
  100.7 0.0 copy-done
  100.7 0.7 copy.8
Async XLA Ops:
  99.0 1.7 %copy-start = (f32[4,128,128]{2,1,0:T(8,128)S(1)}, f32[4,128,128]{2,1,0:T(8,128)}, u32[]{:S(2)}) copy-start(f32[4,128,128]{2,1,0:T(8,128)} %get-tuple-element.5) | copy-start | bytes 786436
